TPU v7x, 32 devices: a whole 2x2x4 slice. The times are simulated.
32 devices in a mesh: outer: 4 (over y, core), inner: 8 (over z, x).
Axes of the slice: x: 2, y: 2, z: 4, core: 2. Of those that a mesh axis runs over, the one named last changes fastest.
Arguments:
- points: float32 [65536, 64], P(('outer', 'inner')), may hold values from -2.5 to 2.5
- charges: float32 [65536, 128], P(('outer', 'inner')), may hold values from -0.4 to 0.4
- interp: float32 [65536, 256], P(('outer', 'inner')), may hold values from -0.25 to 0.25
- order: int32 [65536], P(('outer', 'inner')), may hold values from 0 to 65535, as said below
- near: int32 [128, 8], replicated, may hold values from 0 to 127, as said below
- far: int32 [128, 8], replicated, may hold values from 0 to 127, as said below
- skel: int32 [128, 256], P(('outer', 'inner')), may hold values from 0 to 511, as said below
Outputs:
- potential: float32 [65536, 128], P(('outer', 'inner'))
Inputs may be any that keep to these rules, and one draw needn't show every extreme that they name: `order`: A permutation; tree position p lies on device p // 2048 in the rows' layout, and each device's rows hold exactly 64 positions of every device. `near`: row g names leaf g first, then 8 - 1 distinct leaves on other devices with the same outer index (leaf h lies on device h // 4); the entries of one device's leaves name at most 4 leaves on any one other device, counting repeats, and some pair of devices reaches 4. `far`: row g names 8 distinct leaves on devices with the same inner index as leaf g and another outer index. `skel`: each row holds distinct values.
All inputs are finite; a program needn't handle non-finite values.
Results may differ from a plain program's by a relative error of at most 0.000082.
Values sent between devices are 32-bit elements; how exact they have to be, the bound alone decides.
No kernel may reach another device: no remote copies, remote signals or barrier semaphores. Data moves between devices by JAX's collectives and lax.ppermute only.
A program may use at most 128 MiB of HBM per device.

v0:
```python
import jax
import jax.numpy as jnp
from jax import lax
from jax.sharding import PartitionSpec as P


def apply_tile(target, source, source_chg):
    cross = jnp.dot(
        target, source.T, precision=lax.Precision.HIGHEST, preferred_element_type=jnp.float32
    )
    dist_sq = (
        jnp.sum(target * target, axis=1)[:, None]
        + jnp.sum(source * source, axis=1)[None, :]
        - 2.0 * cross
    )
    kernel = jnp.exp(-dist_sq * (4.0 / target.shape[1]))
    return jnp.dot(
        kernel, source_chg, precision=lax.Precision.HIGHEST, preferred_element_type=jnp.float32
    )


def listed_sum(inputs):
    target, sources, source_chg = inputs
    return jnp.sum(
        jax.vmap(lambda source, charge: apply_tile(target, source, charge))(sources, source_chg),
        axis=0,
    )


def shards(points, charges, interp, order, near, far, skel):
    n_inner = lax.axis_size("inner")
    row_count = points.shape[0]
    leaf_dev = skel.shape[0]
    leaf_size = row_count // leaf_dev
    point_dim = points.shape[1]
    column_count = charges.shape[1]
    outer_idx = lax.axis_index("outer")
    inner_idx = lax.axis_index("inner")
    my_device = outer_idx * n_inner + inner_idx
    sorter = jnp.argsort(order)
    sent_pts = points[sorter]
    sent_chg = charges[sorter]
    slot_pos = (order[sorter] % row_count).astype(jnp.float32)
    got_pts, got_chg, got_pos = (
        lax.all_to_all(sent_pts, ("outer", "inner"), split_axis=0, concat_axis=0, tiled=True),
        lax.all_to_all(sent_chg, ("outer", "inner"), split_axis=0, concat_axis=0, tiled=True),
        lax.all_to_all(slot_pos, ("outer", "inner"), split_axis=0, concat_axis=0, tiled=True),
    )
    positions = got_pos.astype(jnp.int32)
    placer = jnp.argsort(positions)
    leaf_pts = got_pts[placer].reshape(leaf_dev, leaf_size, point_dim)
    leaf_charge_block = got_chg[placer].reshape(leaf_dev, leaf_size, column_count)
    first_leaf = my_device * leaf_dev
    group_first = outer_idx * n_inner * leaf_dev
    near_rows = lax.dynamic_slice_in_dim(near, first_leaf, leaf_dev, 0)
    all_pts, all_chg = (
        lax.all_gather(leaf_pts, "inner", axis=0, tiled=True),
        lax.all_gather(leaf_charge_block, "inner", axis=0, tiled=True),
    )
    picked = near_rows - group_first
    near_pts = all_pts[picked]
    near_chg = all_chg[picked]
    near_part = lax.map(listed_sum, (leaf_pts, near_pts, near_chg))
    leaf_interpolant = interp.reshape(leaf_dev, leaf_size, -1)
    skel_pts = jnp.take_along_axis(leaf_pts, skel[:, :, None], axis=1)
    skeleton_charge = jnp.einsum(
        "euq,eub->eqb", leaf_interpolant, leaf_charge_block, precision=lax.Precision.HIGHEST
    )
    column_pts, column_chg = (
        lax.all_gather(skel_pts, "outer", axis=0, tiled=True),
        lax.all_gather(skeleton_charge, "outer", axis=0, tiled=True),
    )
    far_rows = lax.dynamic_slice_in_dim(far, first_leaf, leaf_dev, 0)
    far_column = far_rows // leaf_dev // n_inner * leaf_dev + far_rows % leaf_dev
    skeleton_potential = lax.map(
        listed_sum, (skel_pts, column_pts[far_column], column_chg[far_column])
    )
    far_field_part = jnp.einsum(
        "izx,ixb->izb", leaf_interpolant, skeleton_potential, precision=lax.Precision.HIGHEST
    )
    tree_pot = (near_part + far_field_part).reshape(row_count, column_count)
    outgoing = tree_pot[positions]
    returned = lax.all_to_all(outgoing, ("outer", "inner"), split_axis=0, concat_axis=0, tiled=True)
    return returned[jnp.argsort(sorter)]


def solution(mesh):
    in_specs = (
        P(("outer", "inner"), None),
        P(("outer", "inner"), None),
        P(("outer", "inner"), None),
        P(("outer", "inner")),
        P(),
        P(),
        P(("outer", "inner"), None),
    )
    out_specs = P(("outer", "inner"), None)
    return jax.shard_map(shards, mesh=mesh, in_specs=in_specs, out_specs=out_specs, check_vma=False)
```

profile of v0, /device:TPU:0, one launch (start us, length us, event | category | flops | bytes accessed | tf_op | source)
XLA Modules:
  0.0 503.3 jit_solution(8625582024046178338)
XLA Ops:
  12.4 11.8 %gather_fusion.1 = s32[2048]{0:T(1024)S(1)} fusion(s32[2048]{0:T(1024)S(1)} %copy-done.1, s32[2048]{0:T(1024)S(1)} %fusion.67), kind=kCustom, calls=%fused_computation.1 | custom fusion | bytes 24576 | tf_op jit(solution)/shard_map/gather | solution.py:43
  33.6 7.6 %gather_fusion = f32[2048,64]{1,0:T(8,128)} fusion(f32[2048,64]{1,0:T(8,128)S(1)} %copy.23, s32[2048]{0:T(1024)S(1)} %fusion.67), kind=kCustom, calls=%fused_computation | custom fusion | bytes 1056768 | tf_op jit(solution)/shard_map/gather | solution.py:41
  50.1 7.6 %gather_fusion.4 = f32[2048,128]{1,0:T(8,128)} fusion(f32[2048,128]{1,0:T(8,128)S(1)} %copy-done.2, s32[2048]{0:T(1024)S(1)} %fusion.67), kind=kCustom, calls=%fused_computation.4 | custom fusion | bytes 2105344 | tf_op jit(solution)/shard_map/gather | solution.py:42
  57.7 8.6 %all-to-all-done = f32[32,1,4096]{2,1,0:T(1,128)} async-done(((f32[32,1,4096]{2,1,0:T(1,128)}), f32[32,1,4096]{2,1,0:T(1,128)}, u32[]{:S(2)}, u32[]{:S(2)}) %all-to-all-start) | async-done | bytes 524320 | tf_op jit(solution)/shard_map/all_to_all | solution.py:45
  80.8 8.8 %gather_fusion.2 = f32[2048,64]{1,0:T(8,128)} fusion(f32[2048,64]{1,0:T(8,128)} %bitcast.147, s32[2048]{0:T(1024)S(1)} %fusion.68), kind=kCustom, calls=%fused_computation.2 | custom fusion | bytes 1056768 | tf_op jit(solution)/shard_map/gather | solution.py:51
  89.6 15.3 %gather_fusion.11 = f32[1024,64]{1,0:T(8,128)} fusion(f32[4,512,64]{2,1,0:T(8,128)} %bitcast.150, s32[1024]{0:T(1024)S(1)} %bitcast.148), kind=kCustom, calls=%fused_computation.11 | custom fusion | bytes 532480 | tf_op jit(solution)/shard_map/jit(take_along_axis)/gather | solution.py:65
  107.0 7.6 %gather_fusion.5 = f32[2048,128]{1,0:T(8,128)} fusion(f32[2048,128]{1,0:T(8,128)S(1)} %bitcast.144, s32[2048]{0:T(1024)S(1)} %fusion.68), kind=kCustom, calls=%fused_computation.5 | custom fusion | bytes 2105344 | tf_op jit(solution)/shard_map/gather | solution.py:52
  128.3 20.9 %all-gather.11.cloned.1.call-done = f32[16,256,128]{2,1,0:T(8,128)} async-done(((f32[4,256,128]{2,1,0:T(8,128)}), f32[16,256,128]{2,1,0:T(8,128)}) %all-gather.11.cloned.1.call-update) | async-done | bytes 2097168 | tf_op jit(solution)/shard_map/all_gather | solution.py:71
  153.6 29.8 %while.21 = (s32[]{:T(128)}, f32[4,256,128]{2,1,0:T(8,128)S(1)}, f32[4,256,64]{1,2,0:T(8,128)S(1)}, f32[4,8,256,64]{2,3,1,0:T(8,128)}, f32[4,8,256,128]{3,2,1,0:T(8,128)}, /*index=5*/s32[]{:T(128)}) while((s32[]{:T(128)}, f32[4,256,128]{2,1,0:T(8,128)S(1)}, f32[4,256,64]{1,2,0:T(8,128)S(1)}, f32[4,8,256,64]{2,3,1,0:T(8,128)}, ...), condition=%wide.region_9.10_spmd, body=%wide.region_6.9_spmd.sunk | while | flops 1210873600 | bytes 6574157 | solution.py:75
  183.4 40.8 %all-gather.5.cloned.1.call-done = f32[32,512,64]{1,2,0:T(8,128)} async-done(((f32[4,512,64]{1,2,0:T(8,128)}), f32[32,512,64]{1,2,0:T(8,128)}) %all-gather.5.cloned.1.call-update) | async-done | bytes 4194320 | tf_op jit(solution)/shard_map/all_gather | solution.py:57
  229.1 120.1 %all-gather.7.cloned.1.call-done = f32[32,512,128]{2,1,0:T(8,128)} async-done(((f32[4,512,128]{2,1,0:T(8,128)}), f32[32,512,128]{2,1,0:T(8,128)}) %all-gather.7.cloned.1.call-update) | async-done | bytes 8388624 | tf_op jit(solution)/shard_map/all_gather | solution.py:58
  349.2 7.7 %gather_fusion.6 = f32[32,512,128]{2,1,0:T(8,128)} fusion(f32[32,512,128]{2,1,0:T(8,128)} %all-gather.7.cloned.1.call-done, s32[1024]{0:T(1024)S(1)} %pad_clamp_fusion.1), kind=kCustom, calls=%fused_computation.6 | custom fusion | bytes 16777344 | tf_op jit(solution)/shard_map/gather | solution.py:62
  356.9 88.2 %while.20 = (s32[]{:T(128)}, f32[4,512,128]{1,2,0:T(8,128)}, f32[4,512,64]{1,2,0:T(8,128)S(1)}, f32[4,8,512,64]{2,3,1,0:T(8,128)}, f32[4,8,512,128]{3,2,1,0:T(8,128)}, /*index=5*/s32[]{:T(128)}) while((s32[]{:T(128)}, f32[4,512,128]{1,2,0:T(8,128)}, f32[4,512,64]{1,2,0:T(8,128)S(1)}, f32[4,8,512,64]{2,3,1,0:T(8,128)}, ...), condition=%wide.region_5.6_spmd, body=%wide.region_2.5_spmd.sunk | while | flops 4842909184 | bytes 21534796 | solution.py:63
  356.9 8.1 %fusion.101 = f32[512,8,512]{2,0,1:T(8,128)S(1)} fusion(f32[4,8,512,64]{2,3,1,0:T(8,128)} %get-tuple-element.181, s32[]{:T(128)} %get-tuple-element.172, f32[4,512,64]{1,2,0:T(8,128)S(1)} %get-tuple-element.180), kind=kOutput, calls=%fused_computation.27.clone.1 | convolution fusion | flops 1610612736 | bytes 9569280 | tf_op jit(solution)/shard_map/while/body/eval_jaxpr/vmap()/dot_general | solution.py:8
  366.4 12.5 %fusion.104 = f32[4,512,128]{1,2,0:T(8,128)} fusion(f32[4,512,128]{1,2,0:T(8,128)} %get-tuple-element.173, s32[]{:T(128)} %get-tuple-element.172, f32[4,8,512,128]{3,2,1,0:T(8,128)} %get-tuple-element.182, f32[512,8,512]{2,0,1:T(8,128)S(1)} %fusion.101, f32[8,512]{1,0:T(8,128)S(1)} %fusion.102, f32[512]{0:T(512)S(1)} %fusion.103), kind=kOutput, calls=%fused_computation.26.clone.1 | convolution fusion | flops 3231711232 | bytes 10767360 | tf_op jit(solution)/shard_map/while/body/eval_jaxpr/vmap()/dot_general | solution.py:17
  379.0 8.1 %fusion.101 = f32[512,8,512]{2,0,1:T(8,128)S(1)} fusion(f32[4,8,512,64]{2,3,1,0:T(8,128)} %get-tuple-element.181, s32[]{:T(128)} %get-tuple-element.172, f32[4,512,64]{1,2,0:T(8,128)S(1)} %get-tuple-element.180), kind=kOutput, calls=%fused_computation.27.clone.1 | convolution fusion | flops 1610612736 | bytes 9569280 | tf_op jit(solution)/shard_map/while/body/eval_jaxpr/vmap()/dot_general | solution.py:8
  388.5 12.5 %fusion.104 = f32[4,512,128]{1,2,0:T(8,128)} fusion(f32[4,512,128]{1,2,0:T(8,128)} %get-tuple-element.173, s32[]{:T(128)} %get-tuple-element.172, f32[4,8,512,128]{3,2,1,0:T(8,128)} %get-tuple-element.182, f32[512,8,512]{2,0,1:T(8,128)S(1)} %fusion.101, f32[8,512]{1,0:T(8,128)S(1)} %fusion.102, f32[512]{0:T(512)S(1)} %fusion.103), kind=kOutput, calls=%fused_computation.26.clone.1 | convolution fusion | flops 3231711232 | bytes 10767360 | tf_op jit(solution)/shard_map/while/body/eval_jaxpr/vmap()/dot_general | solution.py:17
  401.0 8.1 %fusion.101 = f32[512,8,512]{2,0,1:T(8,128)S(1)} fusion(f32[4,8,512,64]{2,3,1,0:T(8,128)} %get-tuple-element.181, s32[]{:T(128)} %get-tuple-element.172, f32[4,512,64]{1,2,0:T(8,128)S(1)} %get-tuple-element.180), kind=kOutput, calls=%fused_computation.27.clone.1 | convolution fusion | flops 1610612736 | bytes 9569280 | tf_op jit(solution)/shard_map/while/body/eval_jaxpr/vmap()/dot_general | solution.py:8
  410.5 12.5 %fusion.104 = f32[4,512,128]{1,2,0:T(8,128)} fusion(f32[4,512,128]{1,2,0:T(8,128)} %get-tuple-element.173, s32[]{:T(128)} %get-tuple-element.172, f32[4,8,512,128]{3,2,1,0:T(8,128)} %get-tuple-element.182, f32[512,8,512]{2,0,1:T(8,128)S(1)} %fusion.101, f32[8,512]{1,0:T(8,128)S(1)} %fusion.102, f32[512]{0:T(512)S(1)} %fusion.103), kind=kOutput, calls=%fused_computation.26.clone.1 | convolution fusion | flops 3231711232 | bytes 10767360 | tf_op jit(solution)/shard_map/while/body/eval_jaxpr/vmap()/dot_general | solution.py:17
  423.1 8.1 %fusion.101 = f32[512,8,512]{2,0,1:T(8,128)S(1)} fusion(f32[4,8,512,64]{2,3,1,0:T(8,128)} %get-tuple-element.181, s32[]{:T(128)} %get-tuple-element.172, f32[4,512,64]{1,2,0:T(8,128)S(1)} %get-tuple-element.180), kind=kOutput, calls=%fused_computation.27.clone.1 | convolution fusion | flops 1610612736 | bytes 9569280 | tf_op jit(solution)/shard_map/while/body/eval_jaxpr/vmap()/dot_general | solution.py:8
  432.6 12.5 %fusion.104 = f32[4,512,128]{1,2,0:T(8,128)} fusion(f32[4,512,128]{1,2,0:T(8,128)} %get-tuple-element.173, s32[]{:T(128)} %get-tuple-element.172, f32[4,8,512,128]{3,2,1,0:T(8,128)} %get-tuple-element.182, f32[512,8,512]{2,0,1:T(8,128)S(1)} %fusion.101, f32[8,512]{1,0:T(8,128)S(1)} %fusion.102, f32[512]{0:T(512)S(1)} %fusion.103), kind=kOutput, calls=%fused_computation.26.clone.1 | convolution fusion | flops 3231711232 | bytes 10767360 | tf_op jit(solution)/shard_map/while/body/eval_jaxpr/vmap()/dot_general | solution.py:17
  451.2 7.6 %gather_fusion.9 = f32[2048,128]{1,0:T(8,128)} fusion(f32[2048,128]{1,0:T(8,128)S(1)} %bitcast.146, s32[2048]{0:T(1024)S(1)} %broadcast_clamp_fusion), kind=kCustom, calls=%fused_computation.9 | custom fusion | bytes 2105344 | tf_op jit(solution)/shard_map/gather | solution.py:82
  466.7 22.4 %all-to-all-done.3 = f32[32,64,128]{2,1,0:T(8,128)S(1)} async-done(((f32[32,64,128]{2,1,0:T(8,128)}), f32[32,64,128]{2,1,0:T(8,128)S(1)}, u32[]{:S(2)}, u32[]{:S(2)}) %all-to-all-start.3) | async-done | bytes 1048608 | tf_op jit(solution)/shard_map/all_to_all | solution.py:83
  489.1 7.6 %gather_fusion.10 = f32[2048,128]{1,0:T(8,128)} fusion(f32[2048,128]{1,0:T(8,128)S(1)} %bitcast.145, s32[2048]{0:T(1024)S(1)} %fusion.69), kind=kCustom, calls=%fused_computation.10 | custom fusion | bytes 2105344 | tf_op jit(solution)/shard_map/gather | solution.py:84
  (101 shorter events, 112.7 us)
Async XLA Ops:
  6.5 108.0 %copy-start = (f32[2048,256]{1,0:T(8,128)S(1)}, f32[2048,256]{1,0:T(8,128)}, u32[]{:S(2)}) copy-start(f32[2048,256]{1,0:T(8,128)} %param.13) | copy-start | bytes 6291460
  6.5 5.9 %copy-start.1 = (s32[2048]{0:T(1024)S(1)}, s32[2048]{0:T(1024)}, u32[]{:S(2)}) copy-start(s32[2048]{0:T(1024)} %param.14) | copy-start | bytes 24580
  24.9 19.1 %all-to-all-start.1 = ((f32[32,64,1]{1,2,0:T(1,128)}), f32[32,64,1]{1,2,0:T(1,128)S(1)}, u32[]{:S(2)}, u32[]{:S(2)}) async-start(f32[32,64,1]{1,2,0:T(1,128)} %bitcast.18), calls=%async_computation.1 | async-start | bytes 32768 | tf_op jit(solution)/shard_map/all_to_all | solution.py:47
  33.6 16.4 %copy-start.6 = (s32[4,256]{1,0:T(4,128)S(1)}, s32[4,256]{1,0:T(4,128)}, u32[]{:S(2)}) copy-start(s32[4,256]{1,0:T(4,128)} %param.17) | copy-start | bytes 12292
  41.3 8.8 %copy-start.2 = (f32[2048,128]{1,0:T(8,128)S(1)}, f32[2048,128]{1,0:T(8,128)}, u32[]{:S(2)}) copy-start(f32[2048,128]{1,0:T(8,128)} %param.12) | copy-start | bytes 3145732
  44.1 22.2 %all-to-all-start = ((f32[32,1,4096]{2,1,0:T(1,128)}), f32[32,1,4096]{2,1,0:T(1,128)}, u32[]{:S(2)}, u32[]{:S(2)}) async-start(f32[32,1,4096]{2,1,0:T(1,128)} %reshape.239), calls=%async_computation | async-start | bytes 1048576 | tf_op jit(solution)/shard_map/all_to_all | solution.py:45
  66.2 40.7 %all-to-all-start.2 = ((f32[32,64,128]{2,1,0:T(8,128)}), f32[32,64,128]{2,1,0:T(8,128)S(1)}, u32[]{:S(2)}, u32[]{:S(2)}) async-start(f32[32,64,128]{2,1,0:T(8,128)} %bitcast.156), calls=%async_computation.2 | async-start | bytes 2097152 | tf_op jit(solution)/shard_map/all_to_all | solution.py:46
  68.9 56.2 %all-gather.9.cloned.1.call-start = ((), (), s32[]{:S(2)}) async-start(), calls=%async_computation.6 | async-start | bytes 1310720 | tf_op jit(solution)/shard_map/all_gather | solution.py:70
  106.9 42.3 %all-gather.11.cloned.1.call-start = ((), (), s32[]{:S(2)}) async-start(), calls=%async_computation.7 | async-start | bytes 2621440 | tf_op jit(solution)/shard_map/all_gather | solution.py:71
  114.6 6.2 %copy-start.3 = (f32[2048,64]{1,0:T(8,128)S(1)}, f32[2048,64]{1,0:T(8,128)}, u32[]{:S(2)}) copy-start(f32[2048,64]{1,0:T(8,128)} %gather_fusion.2) | copy-start | bytes 1572868
  114.6 7.9 %copy-start.7 = (s32[128,8]{0,1:T(8,128)S(1)}, s32[128,8]{0,1:T(8,128)}, u32[]{:S(2)}) copy-start(s32[128,8]{0,1:T(8,128)} %param.16) | copy-start | bytes 12292
  114.6 7.9 %copy-start.8 = (s32[128,8]{0,1:T(8,128)S(1)}, s32[128,8]{0,1:T(8,128)}, u32[]{:S(2)}) copy-start(s32[128,8]{0,1:T(8,128)} %param.15) | copy-start | bytes 12292
  120.7 103.5 %all-gather.5.cloned.1.call-start = ((), (), s32[]{:S(2)}) async-start(), calls=%async_computation.4 | async-start | bytes 4718592 | tf_op jit(solution)/shard_map/all_gather | solution.py:57
  121.9 227.3 %all-gather.7.cloned.1.call-start = ((), (), s32[]{:S(2)}) async-start(), calls=%async_computation.5 | async-start | bytes 9437184 | tf_op jit(solution)/shard_map/all_gather | solution.py:58
  128.3 25.3 %copy-start.5 = (f32[4,256,64]{1,2,0:T(8,128)S(1)}, f32[4,256,64]{1,2,0:T(8,128)}, u32[]{:S(2)}) copy-start(f32[4,256,64]{1,2,0:T(8,128)} %broadcast_select_fusion) | copy-start | bytes 786436
  229.1 127.8 %copy-start.4 = (f32[4,512,64]{1,2,0:T(8,128)S(1)}, f32[4,512,64]{1,2,0:T(8,128)}, u32[]{:S(2)}) copy-start(f32[4,512,64]{1,2,0:T(8,128)} %copy.27) | copy-start | bytes 1572868
  458.8 30.3 %all-to-all-start.3 = ((f32[32,64,128]{2,1,0:T(8,128)}), f32[32,64,128]{2,1,0:T(8,128)S(1)}, u32[]{:S(2)}, u32[]{:S(2)}) async-start(f32[32,64,128]{2,1,0:T(8,128)} %bitcast.157), calls=%async_computation.3 | async-start | bytes 2097152 | tf_op jit(solution)/shard_map/all_to_all | solution.py:83
Sparse Core Ops, SparseCore 0:
  107.0 17.9 all-gather.8
  126.6 22.5 all-gather.10
  151.4 72.7 all-gather.4
  226.2 123.0 all-gather.6
where the time goes:
time: 505 us; the launch traced here: 503 us
  waiting for transfers between devices  215 us (43%)
  matrix products  116 us (23%)
  local copies, waits for them, and re-layouts  108 us (21%)
  other arithmetic  31.4 us (6%)
  starting transfers between devices  19.1 us (4%)
  between operations  13.4 us (3%)
    all_gather x1, waiting for transfers between devices, shards(): lax.all_gather(leaf_charge_block, 'inner', axis=0, tiled=True)  120 us
    dot_general x8, matrix products, apply_tile(): jnp.dot(kernel, source_chg, precision=lax.Precision.HIGHEST, preferred_el...  63.8 us
    dot_general x8, matrix products, apply_tile(): jnp.dot(target, source.T, precision=lax.Precision.HIGHEST, preferred_elem...  43.9 us
    all_gather x1, waiting for transfers between devices, shards(): lax.all_gather(leaf_pts, 'inner', axis=0, tiled=True)  40.8 us
    all_to_all x1, waiting for transfers between devices, shards(): lax.all_to_all(outgoing, ('outer', 'inner'), split_axis=0, concat_axis=0,...  22.4 us
    all_gather x1, waiting for transfers between devices, shards(): lax.all_gather(skeleton_charge, 'outer', axis=0, tiled=True)  20.9 us
    gather x2, local copies, waits for them, and re-layouts, shards(): skel_pts = jnp.take_along_axis(leaf_pts, skel[:, :, None], axis=1)  16.5 us
    gather x2, local copies, waits for them, and re-layouts, shards(): slot_pos = (order[sorter] % row_count).astype(jnp.float32)  11.9 us
  transfers between devices with their start and end apart: 8, of which 6 were waited for; matrix products, arithmetic and copies ran while one was open for 24% of the time, Pallas kernels for 0%

commit v1 on v0

v1 whole, which is shorter than its diff:
```python
import functools
import math

import jax
import jax.numpy as jnp
from jax import lax
from jax.experimental import pallas as pl
from jax.experimental.pallas import tpu as pltpu
from jax.sharding import PartitionSpec as P

F32 = jnp.float32
BF16 = jnp.bfloat16
LANES = 128
JOINT = ("outer", "inner")
VMEM = pl.BlockSpec(memory_space=pltpu.VMEM)
SMEM = pl.BlockSpec(memory_space=pltpu.SMEM)


def call(body, outs, args, in_specs, scratch=(), alias=None, flops=0, name=None, vmem=48):
    nbytes = sum(a.size * 4 for a in args) + sum(o.size * 4 for o in outs)
    return pl.pallas_call(
        body,
        out_shape=outs,
        in_specs=in_specs,
        out_specs=[VMEM] * len(outs),
        scratch_shapes=list(scratch),
        input_output_aliases=alias or {},
        compiler_params=pltpu.CompilerParams(vmem_limit_bytes=vmem << 20),
        cost_estimate=pl.CostEstimate(flops=flops, bytes_accessed=nbytes, transcendentals=0),
        name=name,
    )(*args)


def split(x):
    hi = x.astype(BF16)
    return hi, (x - hi.astype(F32)).astype(BF16)


def split3(x):
    a = x.astype(BF16)
    r = x - a.astype(F32)
    b = r.astype(BF16)
    return a, b, (r - b.astype(F32)).astype(BF16)


def unpack(packed, dim):
    return jnp.concatenate([packed[:, :dim], packed[:, dim : 2 * dim]], axis=0)


def pack(rows, dim):
    half = rows.shape[0] // 2
    return jnp.concatenate([rows[:half, :dim], rows[half:, :dim]], axis=1)


def norm_lanes(x, scale, first):
    n = -scale * jnp.sum(x * x, axis=1, keepdims=True)
    a, b, c = (v.astype(F32) for v in split3(n))
    lane = lax.broadcasted_iota(jnp.int32, x.shape, 1)
    base = 0 if first else 3
    ones = 3 if first else 0
    out = jnp.where((lane >= ones) & (lane < ones + 3), 1.0, 0.0)
    for j, v in enumerate((a, b, c)):
        out = jnp.where(lane == base + j, v, out)
    return out.astype(BF16)


def target_side(x, scale):
    hi, lo = split(x * (2.0 * scale))
    return jnp.concatenate([hi, lo, hi, norm_lanes(x, scale, True)], axis=1)


def source_side(x, scale):
    hi, lo = split(x)
    return jnp.concatenate([hi, hi, lo, norm_lanes(x, scale, False)], axis=1)


def charge_side(c):
    hi, lo = split(c)
    return jnp.concatenate([hi, lo], axis=1)


def nt_dot(a, b):
    return lax.dot_general(a, b, (((1,), (1,)), ((), ())), preferred_element_type=F32)


def tn_dot(a, b):
    return lax.dot_general(a, b, (((0,), (0,)), ((), ())), preferred_element_type=F32)


def fold(p):
    half = p.shape[1] // 2
    return p[:, :half] + p[:, half:]


def tile_product(target, source, charge):
    k = jnp.exp2(nt_dot(target, source))
    hi, lo = split(k)
    return fold(
        jnp.dot(hi, charge, preferred_element_type=F32)
        + jnp.dot(lo, charge, preferred_element_type=F32)
    )


def div_mod(x, n):
    if n & (n - 1) == 0:
        return lax.shift_right_logical(x, jnp.int32(n.bit_length() - 1)), x & (n - 1)
    q = lax.div(x, jnp.int32(n))
    return q, x - q * n


UNROLL = 16


def rows_loop(count, body):
    def step(i, carry):
        for u in range(UNROLL):
            body(i * UNROLL + u)
        return carry

    lax.fori_loop(0, count // UNROLL, step, 0)


def send_kernel(devs, pair, block, order_ref, pts_ref, chg_ref, send_ref, code_ref, ptmp, idx_v, idx_s, sem):
    rows = chg_ref.shape[0]
    dim = pts_ref.shape[1]
    lines = rows // LANES
    dest, slot = div_mod(order_ref[...], rows)
    sub = lax.broadcasted_iota(jnp.int32, (devs, LANES), 0)
    hot = [jnp.where(dest[r : r + 1, :] == sub, 1.0, 0.0) for r in range(lines)]
    ki = lax.broadcasted_iota(jnp.int32, (LANES, 2 * LANES), 0)
    ji = lax.broadcasted_iota(jnp.int32, (LANES, 2 * LANES), 1)
    tri = jnp.where((ki < ji) | (ji >= LANES), 1.0, 0.0).astype(BF16)
    pre = jnp.dot(jnp.concatenate([h.astype(BF16) for h in hot], axis=0), tri, preferred_element_type=F32)
    base = jnp.zeros((devs, LANES), F32)
    ranks = []
    for r in range(lines):
        part = pre[r * devs : (r + 1) * devs]
        ranks.append(jnp.sum(hot[r] * (part[:, :LANES] + base), axis=0, keepdims=True))
        base = base + part[:, LANES:]
    rank_f = jnp.concatenate(ranks, axis=0)
    rank = rank_f.astype(jnp.int32)
    idx_v[...] = dest * block + rank
    copy = pltpu.make_async_copy(idx_v, idx_s, sem)
    copy.start()
    code_ref[...] = dest * (2 * pair) + rank
    psub = lax.broadcasted_iota(jnp.int32, (pair, LANES), 0)
    s_hi = lax.shift_right_logical(slot, 8).astype(F32)
    s_lo = (slot & 255).astype(F32)
    left, right = [], []
    for r in range(lines):
        left.append(
            jnp.concatenate([hot[r] * s_hi[r : r + 1, :], hot[r] * s_lo[r : r + 1, :]], axis=0).astype(BF16)
        )
        right.append(jnp.where(rank[r : r + 1, :] == psub, 1.0, 0.0).astype(BF16))
    both = nt_dot(jnp.concatenate(left, axis=1), jnp.concatenate(right, axis=1))
    table = both[:devs] * 256.0 + both[devs:]
    if pair < LANES:
        table = jnp.concatenate([table, jnp.zeros((devs, LANES - pair), F32)], axis=1)
    copy.wait()

    def move(n):
        j = idx_s[n // LANES, n % LANES]
        send_ref[pl.ds(j, 1), :] = chg_ref[pl.ds(n, 1), :]
        ptmp[pl.ds(j, 1), :dim] = pts_ref[pl.ds(n, 1), :]

    rows_loop(rows, move)
    half = pair // 2
    for d in range(devs):
        send_ref[d * block + pair : d * block + pair + half, :] = pack(
            ptmp[d * block : d * block + pair, :], dim
        )
        send_ref[d * block + pair + half : (d + 1) * block, :] = jnp.broadcast_to(
            table[d : d + 1, :], (block - pair - half, LANES)
        )


def place_kernel(devs, pair, block, leaf, dim, recv_ref, ring_ref, pts_ref, exch_ref, pos_ref, rolled, pos_s, sem):
    half = pair // 2
    rows = pts_ref.shape[0]
    leaves = rows // leaf
    line = leaf + leaf // 2
    table = jnp.concatenate(
        [recv_ref[d * block + pair + half : d * block + pair + half + 1, :] for d in range(devs)], axis=0
    )
    pos_ref[...] = table.astype(jnp.int32)
    copy = pltpu.make_async_copy(pos_ref, pos_s, sem)
    copy.start()
    exch_ref[rows // 2 :, :] = table
    for d in range(devs):
        part = recv_ref[d * block + pair : d * block + pair + half, :]
        rolled[d * half : (d + 1) * half, :] = jnp.concatenate([part[:, dim:], part[:, :dim]], axis=1)
    copy.wait()

    def per_source(d, carry):
        for j in range(pair):
            p = pos_s[d, j]
            g, _ = div_mod(p, leaf)
            ring_ref[pl.ds(p + g * (line - leaf), 1), :] = recv_ref[pl.ds(d * block + j, 1), :]
            if j < half:
                pts_ref[pl.ds(p, 1), :] = recv_ref[pl.ds(d * block + pair + j, 1), :]
            else:
                pts_ref[pl.ds(p, 1), :] = rolled[pl.ds(d * half + j - half, 1), :]
        return carry

    lax.fori_loop(0, devs, per_source, 0)
    for g in range(leaves):
        packed = pack(pts_ref[g * leaf : (g + 1) * leaf, :], dim)
        ring_ref[g * line + leaf : (g + 1) * line, :] = packed
        exch_ref[g * (leaf // 2) : (g + 1) * (leaf // 2), :] = packed


def skeleton_kernel(leaf, dim, ring_ref, pts_ref, interp_ref, skel_ref, far_ref, stmp):
    leaves, skel = skel_ref.shape
    line = leaf + leaf // 2
    fline = skel + skel // 2

    for g in range(leaves):

        def move(n, g=g):
            stmp[pl.ds(g * skel + n, 1), :] = pts_ref[pl.ds(g * leaf + skel_ref[g, n], 1), :]

        rows_loop(skel, move)
    for g in range(leaves):
        hi, lo = split(interp_ref[g * leaf : (g + 1) * leaf, :])
        charge = charge_side(ring_ref[g * line : g * line + leaf, :])
        far_ref[g * fline : g * fline + skel, :] = fold(tn_dot(hi, charge) + tn_dot(lo, charge))
        far_ref[g * fline + skel : (g + 1) * fline, :] = pack(stmp[g * skel : (g + 1) * skel, :], dim)


def far_kernel(skel, dim, scale, n_inner, blocks, far_rows_ref, own_ref, interp_ref, *rest):
    refs, (out_ref, src, chg) = rest[:blocks], rest[blocks:]
    leaves, fars = far_rows_ref.shape
    leaf = interp_ref.shape[0] // leaves
    fline = skel + skel // 2
    outer = lax.axis_index("outer")
    for b in range(blocks):
        for g in range(leaves):
            at = b * leaves + g
            src[at] = source_side(unpack(refs[b][g * fline + skel : (g + 1) * fline, :], dim), scale)
            chg[at] = charge_side(refs[b][g * fline : g * fline + skel, :])

    for g in range(leaves):
        target = target_side(unpack(own_ref[g * fline + skel : (g + 1) * fline, :], dim), scale)
        q = jnp.zeros((skel, LANES), F32)
        for k in range(fars):
            device, local = div_mod(far_rows_ref[g, k], leaves)
            at = ((device // n_inner) ^ outer) * leaves - leaves + local
            q = q + tile_product(target, src[at], chg[at])
        qq = charge_side(q)
        hi, lo = split(interp_ref[g * leaf : (g + 1) * leaf, :])
        out_ref[g * leaf : (g + 1) * leaf, :] = fold(
            jnp.dot(hi, qq, preferred_element_type=F32) + jnp.dot(lo, qq, preferred_element_type=F32)
        )


def target_kernel(leaf, dim, scale, packed_ref, out_ref):
    for g in range(out_ref.shape[0]):
        x = unpack(packed_ref[g * (leaf // 2) : (g + 1) * (leaf // 2), :], dim)
        out_ref[g] = target_side(x, scale)


def near_kernel(leaf, dim, scale, leaves, parts, fresh, *refs):
    near_ref, who_ref, own_ref, partner_ref = refs[:4]
    sources = refs[4 : 4 + len(parts)]
    rest = refs[4 + len(parts) :]
    acc_ref, src, chg = rest[-3:]
    line = leaf + leaf // 2
    n_near = near_ref.shape[1]
    at = 0
    for ref, (first, count) in zip(sources, parts):
        for g in range(count):
            src[at + g] = source_side(unpack(ref[g * line + leaf : (g + 1) * line, :], dim), scale)
            chg[at + g] = charge_side(ref[g * line : g * line + leaf, :])
        at += count
    acc_ref[...] = jnp.zeros_like(acc_ref) if fresh else rest[0][...]

    step = leaf // 2

    def one(side, target_ref, t, k):
        device, local = div_mod(near_ref[side * leaves + t, k], leaves)
        at = 0
        for b, (first, count) in enumerate(parts):
            hit = (device == who_ref[b]) & (local >= first) & (local < first + count)
            index = at - first + local
            at += count

            @pl.when(hit)
            def _():
                for c in range(0, leaf, step):
                    rows = pl.ds(pl.multiple_of((side * leaves + t) * leaf + c, step), step)
                    acc_ref[rows, :] += tile_product(
                        target_ref[t, c : c + step, :], src[index], chg[index]
                    )

    for side, target_ref in enumerate((own_ref, partner_ref)):

        def entry(e, carry, side=side, target_ref=target_ref):
            t, k = div_mod(e, n_near)
            one(side, target_ref, t, k)
            return carry

        lax.fori_loop(0, leaves * n_near, entry, 0)


def return_kernel(devs, pair, acc_ref, far_ref, pos_ref, other_ref, out_ref, total, opos_v, opos_s, sem):
    rows = far_ref.shape[0]
    opos_v[...] = other_ref[...].astype(jnp.int32)
    copy = pltpu.make_async_copy(opos_v, opos_s, sem)
    copy.start()
    total[...] = acc_ref[:rows, :] + far_ref[...]
    copy.wait()

    def per_source(d, carry):
        for j in range(pair):
            out_ref[pl.ds(d * 2 * pair + j, 1), :] = total[pl.ds(pos_ref[d, j], 1), :]
            out_ref[pl.ds(d * 2 * pair + pair + j, 1), :] = acc_ref[pl.ds(rows + opos_s[d, j], 1), :]
        return carry

    lax.fori_loop(0, devs, per_source, 0)


def final_kernel(pair, n_inner, ret_ref, code_ref, out_ref):
    flip = (n_inner // 2) * 2 * pair

    def move(n):
        c = code_ref[n // LANES, n % LANES]
        out_ref[pl.ds(n, 1), :] = ret_ref[pl.ds(c, 1), :] + ret_ref[pl.ds((c ^ flip) + pair, 1), :]

    rows_loop(out_ref.shape[0], move)


def shards(points, charges, interp, order, near, far, skel):
    n_inner = lax.axis_size("inner")
    n_outer = lax.axis_size("outer")
    devs = n_inner * n_outer
    rows, dim = points.shape
    leaves, n_skel = skel.shape
    leaf = rows // leaves
    line = leaf + leaf // 2
    fline = n_skel + n_skel // 2
    pair = rows // devs
    block = pair + pair // 2 + 8
    scale = (4.0 / dim) * math.log2(math.e)
    outer = lax.axis_index("outer")
    inner = lax.axis_index("inner")
    me = outer * n_inner + inner
    half = n_inner // 2
    partner = outer * n_inner + (inner ^ half)

    def f32(*shape):
        return jax.ShapeDtypeStruct(shape, F32)

    def i32(*shape):
        return jax.ShapeDtypeStruct(shape, jnp.int32)

    def near_of(device):
        return lax.dynamic_slice_in_dim(near, device * leaves, leaves, 0)

    near_rows = jnp.concatenate([near_of(me), near_of(partner)], axis=0)
    far_rows = lax.dynamic_slice_in_dim(far, me * leaves, leaves, 0)

    send, code = call(
        functools.partial(send_kernel, devs, pair, block),
        [f32(devs * block, LANES), i32(rows // LANES, LANES)],
        (order.reshape(rows // LANES, LANES), points, charges),
        [VMEM] * 3,
        [
            pltpu.VMEM((devs * block, LANES), F32),
            pltpu.VMEM((rows // LANES, LANES), jnp.int32),
            pltpu.SMEM((rows // LANES, LANES), jnp.int32),
            pltpu.SemaphoreType.DMA,
        ],
        name="send",
    )
    recv = lax.all_to_all(send.reshape(devs, block, LANES), JOINT, 0, 0, tiled=True)
    ring, pts, exch, pos = call(
        functools.partial(place_kernel, devs, pair, block, leaf, dim),
        [f32(leaves * line, LANES), f32(rows, LANES), f32(rows // 2 + devs, LANES), i32(devs, LANES)],
        (recv.reshape(devs * block, LANES),),
        [VMEM],
        [
            pltpu.VMEM((devs * pair // 2, LANES), F32),
            pltpu.SMEM((devs, LANES), jnp.int32),
            pltpu.SemaphoreType.DMA,
        ],
        name="place",
    )

    loop = [j ^ (j >> 1) for j in range(half)]
    right = [
        (base + loop[j], base + loop[(j + 1) % half]) for base in (0, half) for j in range(half)
    ]
    left = [(b, a) for a, b in right]
    place_of = jnp.asarray([loop.index(j % half) for j in range(n_inner)], jnp.int32)
    member = jnp.asarray(loop, jnp.int32)

    def owner(offset):
        at = place_of[inner] + offset
        return outer * n_inner + (inner // half) * half + member[at % half]

    from_left, from_right = ring, ring
    arrivals = []
    for step in range(1, half // 2):
        from_left = lax.ppermute(from_left, "inner", right)
        from_right = lax.ppermute(from_right, "inner", left)
        arrivals.append((((from_left, 0, leaves, -step),), ((from_right, 0, leaves, step),)))
    theirs = lax.ppermute(exch, "inner", [(i, i ^ half) for i in range(n_inner)])
    cut = leaves // 2
    low = lax.ppermute(from_left[: cut * line], "inner", right)
    high = lax.ppermute(from_right[cut * line :], "inner", left)

    (far_own,) = call(
        functools.partial(skeleton_kernel, leaf, dim),
        [f32(leaves * fline, LANES)],
        (ring, pts, interp, skel),
        [VMEM, VMEM, VMEM, SMEM],
        [pltpu.VMEM((leaves * n_skel, LANES), F32)],
        flops=2 * rows * n_skel * 3 * 128,
        name="skeleton",
    )
    held = {0: far_own}
    bit = n_outer // 2
    while bit:
        perm = [(o, o ^ bit) for o in range(n_outer)]
        held.update({r ^ bit: lax.ppermute(v, "outer", perm) for r, v in list(held.items())})
        bit //= 2

    targets = []
    for packed in (exch, theirs):
        (t,) = call(
            functools.partial(target_kernel, leaf, dim, scale),
            [jax.ShapeDtypeStruct((leaves, leaf, 4 * dim), BF16)],
            (packed,),
            [VMEM],
            name="targets",
        )
        targets.append(t)

    def near_call(acc, pieces):
        parts = tuple((first, count) for _, first, count, _ in pieces)
        who = jnp.stack([owner(offset) for _, _, _, offset in pieces])
        total = sum(count for _, count in parts)
        args = (near_rows, who, *targets, *(p[0] for p in pieces))
        specs = [SMEM, SMEM] + [VMEM] * (2 + len(pieces))
        alias = {}
        if acc is not None:
            alias = {len(args): 0}
            args += (acc,)
            specs.append(VMEM)
        return call(
            functools.partial(near_kernel, leaf, dim, scale, leaves, parts, acc is None),
            [f32(2 * rows, LANES)],
            args,
            specs,
            [
                pltpu.VMEM((total, leaf, 4 * dim), BF16),
                pltpu.VMEM((total, leaf, 2 * LANES), BF16),
            ],
            alias,
            flops=total * 2 * leaf * leaf * 256 * 3 * 2,
            name="near",
        )[0]

    acc = near_call(None, ((ring, 0, leaves, 0),))
    for a, b in arrivals:
        acc = near_call(acc, a)
        acc = near_call(acc, b)
    others = [held[r] for r in range(1, n_outer)]
    n_blocks = len(others) * leaves
    (far_part,) = call(
        functools.partial(far_kernel, n_skel, dim, scale, n_inner, len(others)),
        [f32(rows, LANES)],
        (far_rows, far_own, interp, *others),
        [SMEM] + [VMEM] * (2 + len(others)),
        [
            pltpu.VMEM((n_blocks, n_skel, 4 * dim), BF16),
            pltpu.VMEM((n_blocks, n_skel, 2 * LANES), BF16),
        ],
        flops=leaves * 8 * 2 * n_skel * n_skel * 256 * 3,
        name="far",
    )
    opposite = half // 2
    acc = near_call(acc, ((low, 0, cut, opposite), (high, cut, leaves - cut, opposite)))

    (out,) = call(
        functools.partial(return_kernel, devs, pair),
        [f32(devs * 2 * pair, LANES)],
        (acc, far_part, pos, theirs[rows // 2 :]),
        [VMEM, VMEM, SMEM, VMEM],
        [
            pltpu.VMEM((rows, LANES), F32),
            pltpu.VMEM((devs, LANES), jnp.int32),
            pltpu.SMEM((devs, LANES), jnp.int32),
            pltpu.SemaphoreType.DMA,
        ],
        name="outgoing",
    )
    returned = lax.all_to_all(out.reshape(devs, 2 * pair, LANES), JOINT, 0, 0, tiled=True)
    (final,) = call(
        functools.partial(final_kernel, pair, n_inner),
        [f32(rows, LANES)],
        (returned.reshape(devs * 2 * pair, LANES), code),
        [VMEM, SMEM],
        name="final",
    )
    return final


def solution(mesh):
    row = P(JOINT, None)
    in_specs = (row, row, row, P(JOINT), P(), P(), row)
    return jax.shard_map(shards, mesh=mesh, in_specs=in_specs, out_specs=row, check_vma=False)
```

time: 505 us -> 249 us (0.49)
  waiting for transfers between devices: 215 us -> 29.4 us
  matrix products: 116 us -> 0 us
  blocking collectives: 0 us -> 102 us
  local copies, waits for them, and re-layouts: 108 us -> 6.18 us
  Pallas kernels: 0 us -> 96.9 us
  other arithmetic: 31.4 us -> 0.08 us
  starting transfers between devices: 19.1 us -> 6.56 us
  between operations: 13.4 us -> 6.68 us
    all_gather x4 -> x0, waiting for transfers between devices: 184 us -> none  [the longest x1 120 us: shards(): lax.all_gather(leaf_charge_block, 'inner', axis=0, tiled=True)]
    dot_general x18 -> x0, matrix products: 116 us -> none  [the longest x8 63.8 us: apply_tile(): jnp.dot(kernel, source_chg, precision=lax.Precision.HIGHEST, preferred_el...]
    all_to_all x0 -> x2, blocking collectives: none -> 102 us  [the longest x1 53.8 us: shards(): lax.all_to_all(out.reshape(devs, 2 * pair, LANES), JOINT, 0, 0, tiled=True)]
    pallas_call x0 -> x12, Pallas kernels: none -> 96.9 us  [call(): pl.pallas_call(body, out_shape=outs, in_specs=in_specs, out_specs=[VMEM]...]
    gather x14 -> x0, local copies, waits for them, and re-layouts: 95.4 us -> none  [the longest x2 16.5 us: shards(): skel_pts = jnp.take_along_axis(leaf_pts, skel[:, :, None], axis=1)]
    all_to_all x4 -> x0, waiting for transfers between devices: 31 us -> none  [the longest x1 22.4 us: shards(): lax.all_to_all(outgoing, ('outer', 'inner'), split_axis=0, concat_axis=0,...]
    ppermute x0 -> x8, waiting for transfers between devices: none -> 29.4 us  [the longest x1 29.3 us: shards(): lax.ppermute(exch, 'inner', [(i, i ^ half) for i in range(n_inner)])]
    all_to_all x4 -> x0, starting transfers between devices: 18.7 us -> none  [the longest x1 7.33 us: shards(): lax.all_to_all(slot_pos, ('outer', 'inner'), split_axis=0, concat_axis=0,...]
  transfers between devices with their start and end apart: 8 -> 8, of which waited for: 6 -> 1; matrix products, arithmetic and copies ran while one was open for 24% -> 2% of each run, Pallas kernels for 0% -> 17%
where the time goes in v1:
time: 249 us; the launch traced here: 248 us
  blocking collectives  102 us (41%)
  Pallas kernels  96.9 us (39%)
  waiting for transfers between devices  29.4 us (12%)
  between operations  6.68 us (3%)
  starting transfers between devices  6.56 us (3%)
  local copies, waits for them, and re-layouts  6.18 us (2%)
    pallas_call x12, Pallas kernels, call(): pl.pallas_call(body, out_shape=outs, in_specs=in_specs, out_specs=[VMEM]...  96.9 us
    all_to_all x1, blocking collectives, shards(): lax.all_to_all(out.reshape(devs, 2 * pair, LANES), JOINT, 0, 0, tiled=True)  53.8 us
    all_to_all x1, blocking collectives, shards(): lax.all_to_all(send.reshape(devs, block, LANES), JOINT, 0, 0, tiled=True)  48.6 us
    ppermute x1, waiting for transfers between devices, shards(): lax.ppermute(exch, 'inner', [(i, i ^ half) for i in range(n_inner)])  29.3 us
  transfers between devices with their start and end apart: 8, of which 1 were waited for; matrix products, arithmetic and copies ran while one was open for 2% of the time, Pallas kernels for 17%

profile of v1, /device:TPU:0, one launch (start us, length us, event | category | flops | bytes accessed | tf_op | source)
XLA Modules:
  0.0 248.1 jit_solution(4306496121230557997)
XLA Ops:
  0.0 1.5 copy.15.pts_ref
  1.5 0.7 copy-done.3
  2.2 16.9 %send.1 = (f32[3328,128]{1,0:T(8,128)S(1)}, s32[16,128]{1,0:T(8,128)S(1)}) custom-call(s32[16,128]{1,0:T(8,128)S(1)} %bitcast.18, f32[2048,64]{1,0:T(8,128)S(1)} %copy.15.pts_ref, f32[2048,128]{1,0:T(8,128)S(1)} %copy-done.2), custom_call_target="tpu_custom_call" | custom-call | bytes 3293184 | tf_op jit(solution)/shard_map/send/pallas_call | solution.py:21
  19.2 48.6 %all_to_all.10 = f32[32,104,128]{2,1,0:T(8,128)S(1)} all-to-all(f32[32,104,128]{2,1,0:T(8,128)S(1)} %bitcast.17), channel_id=1, replica_groups=mesh['outer'=4,'inner'=8] {'outer','inner'}, dimensions={0} | all-to-all | bytes 3407872 | tf_op jit(solution)/shard_map/all_to_all | solution.py:375
  67.8 6.3 %place.1 = (f32[3072,128]{1,0:T(8,128)}, f32[2048,128]{1,0:T(8,128)S(1)}, f32[1056,128]{1,0:T(8,128)S(1)}, s32[32,128]{1,0:T(8,128)S(1)}) custom-call(f32[3328,128]{1,0:T(8,128)S(1)} %bitcast.16), custom_call_target="tpu_custom_call" | custom-call | bytes 4882432 | tf_op jit(solution)/shard_map/place/pallas_call | solution.py:21
  74.1 0.7 collective-permute-start.3
  74.8 1.3 collective-permute-start.1
  76.2 4.7 %skeleton.1.own_ref = f32[1536,128]{1,0:T(8,128)S(1)} custom-call(f32[3072,128]{1,0:T(8,128)} %get-tuple-element.13.refs_4_.ring_ref, f32[2048,128]{1,0:T(8,128)S(1)} %get-tuple-element.14.pts_ref, f32[2048,256]{1,0:T(8,128)S(1)} %copy-done.1, s32[4,256]{1,0:T(4,128)S(1)} %copy-done.4), custom_call_target="tpu_custom_call" | custom-call | flops 402653184 | bytes 5509120 | tf_op jit(solution)/shard_map/skeleton/pallas_call | solution.py:21
  80.8 0.6 collective-permute-start.6
  86.6 0.6 fusion
  90.2 0.9 targets.2.refs_2_
  91.2 29.3 %collective-permute-done.packed_ref = f32[1056,128]{1,0:T(8,128)S(1)} collective-permute-done((f32[1056,128]{1,0:T(8,128)S(1)}, f32[1056,128]{1,0:T(8,128)S(1)}, u32[]{:S(2)}, u32[]{:S(2)}) %collective-permute-start) | collective-permute-done | bytes 540704 | tf_op jit(solution)/shard_map/ppermute | solution.py:407
  120.5 0.9 targets.3.refs_3_
  121.6 8.5 %near.4.refs_5_ = f32[4096,128]{1,0:T(8,128)S(1)} custom-call(s32[8,8]{1,0:T(8,128)S(1)} %pad_add_fusion.refs_0_, s32[1]{0:T(128)} %bitcast.11.refs_1_, bf16[4,512,256]{2,1,0:T(8,128)(2,1)S(1)} %targets.2.refs_2_, bf16[4,512,256]{2,1,0:T(8,128)(2,1)S(1)} %targets.3.refs_3_, f32[3072,128]{1,0:T(8,128)} %get-tuple-element.13.refs_4_.ring_ref), custom_call_target="tpu_custom_call" | custom-call | flops 3221225472 | bytes 7864580 | tf_op jit(solution)/shard_map/near/pallas_call | solution.py:21
  130.1 1.2 slice.13
  131.3 3.1 %collective-permute-start.4 = (f32[1536,128]{1,0:T(8,128)S(1)}, f32[1536,128]{1,0:T(8,128)S(1)}, u32[]{:S(2)}, u32[]{:S(2)}) collective-permute-start(f32[1536,128]{1,0:T(8,128)S(1)} %slice.13), channel_id=1, source_target_pairs={{1,0},{3,1},{2,3},{0,2},{5,4},{7,5},{6,7},{4,6},{9,8},{11,9},{10,1... | collective-permute-start | bytes 2359304 | tf_op jit(solution)/shard_map/ppermute | solution.py:410
  134.5 1.2 slice.12
  135.7 9.0 %near.5.refs_5_ = f32[4096,128]{1,0:T(8,128)S(1)} custom-call(s32[8,8]{1,0:T(8,128)S(1)} %pad_add_fusion.refs_0_, s32[1]{0:T(128)} %bitcast.9.refs_1_, bf16[4,512,256]{2,1,0:T(8,128)(2,1)S(1)} %targets.2.refs_2_, bf16[4,512,256]{2,1,0:T(8,128)(2,1)S(1)} %targets.3.refs_3_, ...), custom_call_target="tpu_custom_call", output_to_operand_aliasing={{}: (5, {})} | custom-call | flops 3221225472 | bytes 9961732 | tf_op jit(solution)/shard_map/near/pallas_call | solution.py:21
  144.7 8.8 %near.6.refs_6_ = f32[4096,128]{1,0:T(8,128)S(1)} custom-call(s32[8,8]{1,0:T(8,128)S(1)} %pad_add_fusion.refs_0_, s32[1]{0:T(128)} %bitcast.7.refs_1_, bf16[4,512,256]{2,1,0:T(8,128)(2,1)S(1)} %targets.2.refs_2_, bf16[4,512,256]{2,1,0:T(8,128)(2,1)S(1)} %targets.3.refs_3_, ...), custom_call_target="tpu_custom_call", output_to_operand_aliasing={{}: (5, {})} | custom-call | flops 3221225472 | bytes 9961732 | tf_op jit(solution)/shard_map/near/pallas_call | solution.py:21
  153.5 9.7 %far.1.far_ref = f32[2048,128]{1,0:T(8,128)S(1)} custom-call(s32[4,8]{1,0:T(4,128)S(1)} %copy.19.far_rows_ref, f32[1536,128]{1,0:T(8,128)S(1)} %skeleton.1.own_ref, f32[2048,256]{1,0:T(8,128)} %interp_ref.3, f32[1536,128]{1,0:T(8,128)S(1)} %collective-permute-done.5.rest_0_, f32[1536,128]{1,0:T(8,128)S(1)} %collective-permute-done.6.rest_1_, ...), custom_call_target="tpu_custom_call" | custom-call | flops 3221225472 | bytes 6291584 | tf_op jit(solution)/shard_map/far/pallas_call | solution.py:21
  163.2 8.5 %near.7.acc_ref = f32[4096,128]{1,0:T(8,128)S(1)} custom-call(s32[8,8]{1,0:T(8,128)S(1)} %pad_add_fusion.refs_0_, s32[2]{0:T(128)S(1)} %pad_add_fusion.1.refs_1_, bf16[4,512,256]{2,1,0:T(8,128)(2,1)S(1)} %targets.2.refs_2_, bf16[4,512,256]{2,1,0:T(8,128)(2,1)S(1)} %targets.3.refs_3_, ...), custom_call_target="tpu_custom_call", output_to_operand_aliasing={{}: (6, {})} | custom-call | flops 3221225472 | bytes 9961736 | tf_op jit(solution)/shard_map/near/pallas_call | solution.py:21
  171.8 4.4 %outgoing.1 = f32[4096,128]{1,0:T(8,128)S(1)} custom-call(f32[4096,128]{1,0:T(8,128)S(1)} %near.7.acc_ref, f32[2048,128]{1,0:T(8,128)S(1)} %far.1.far_ref, s32[32,128]{1,0:T(8,128)S(1)} %get-tuple-element.15.pos_ref, f32[32,128]{1,0:T(8,128)S(1)} %slice.14.other_ref), custom_call_target="tpu_custom_call" | custom-call | bytes 5275648 | tf_op jit(solution)/shard_map/outgoing/pallas_call | solution.py:21
  176.2 53.8 %all_to_all.11 = f32[32,128,128]{2,1,0:T(8,128)S(1)} all-to-all(f32[32,128,128]{2,1,0:T(8,128)S(1)} %bitcast.14), channel_id=1, replica_groups=mesh['outer'=4,'inner'=8] {'outer','inner'}, dimensions={0} | all-to-all | bytes 4194304 | tf_op jit(solution)/shard_map/all_to_all | solution.py:498
  230.0 18.1 %final.1 = f32[2048,128]{1,0:T(8,128)} custom-call(f32[4096,128]{1,0:T(8,128)S(1)} %bitcast.15, s32[16,128]{1,0:T(8,128)S(1)} %get-tuple-element.16.code_ref), custom_call_target="tpu_custom_call" | custom-call | bytes 3153920 | tf_op jit(solution)/shard_map/final/pallas_call | solution.py:21
  (35 shorter events, 1.9 us)
Async XLA Ops:
  0.0 89.7 %copy-start = (s32[128,8]{0,1:T(8,128)S(1)}, s32[128,8]{0,1:T(8,128)}, u32[]{:S(2)}) copy-start(s32[128,8]{0,1:T(8,128)} %param.14) | copy-start | bytes 12292
  0.0 1.5 copy-start.2
  1.5 0.7 copy-start.3
  19.1 57.0 %copy-start.1 = (f32[2048,256]{1,0:T(8,128)S(1)}, f32[2048,256]{1,0:T(8,128)}, u32[]{:S(2)}) copy-start(f32[2048,256]{1,0:T(8,128)} %interp_ref.3) | copy-start | bytes 6291460
  19.1 57.0 %copy-start.4 = (s32[4,256]{1,0:T(4,128)S(1)}, s32[4,256]{1,0:T(4,128)}, u32[]{:S(2)}) copy-start(s32[4,256]{1,0:T(4,128)} %skel_ref.1) | copy-start | bytes 12292
  74.1 56.1 %collective-permute-start.3 = (f32[3072,128]{1,0:T(8,128)}, f32[3072,128]{1,0:T(8,128)}, u32[]{:S(2)}, u32[]{:S(2)}) collective-permute-start(f32[3072,128]{1,0:T(8,128)} %get-tuple-element.13.refs_4_.ring_ref), channel_id=1, source_target_pairs={{1,0},{3,1},{2,3},{0,2},{5,4},{7,5},{6,7},{4,6},{9,8},{11,9},{10,1... | collective-permute-start | bytes 4718600 | tf_op jit(solution)/shard_map/ppermute | solution.py:405
  74.8 59.6 %collective-permute-start.1 = (f32[3072,128]{1,0:T(8,128)}, f32[3072,128]{1,0:T(8,128)}, u32[]{:S(2)}, u32[]{:S(2)}) collective-permute-start(f32[3072,128]{1,0:T(8,128)} %get-tuple-element.13.refs_4_.ring_ref), channel_id=1, source_target_pairs={{0,1},{1,3},{3,2},{2,0},{4,5},{5,7},{7,6},{6,4},{8,9},{9,11},{11,1... | collective-permute-start | bytes 4718600 | tf_op jit(solution)/shard_map/ppermute | solution.py:404
  76.1 5.9 %copy-start.7 = (s32[8]{0:T(128)S(1)}, s32[8]{0:T(128)}, u32[]{:S(2)}) copy-start(s32[8]{0:T(128)} %constant.68.clone) | copy-start | bytes 100
  76.1 10.4 %copy-start.6 = (s32[4]{0:T(128)S(1)}, s32[4]{0:T(128)}, u32[]{:S(2)}) copy-start(s32[4]{0:T(128)} %constant.69.clone) | copy-start | bytes 52
  76.2 13.7 %copy-start.5 = (s32[128,8]{0,1:T(8,128)S(1)}, s32[128,8]{0,1:T(8,128)}, u32[]{:S(2)}) copy-start(s32[128,8]{0,1:T(8,128)} %param.13) | copy-start | bytes 12292
  80.8 40.6 %collective-permute-start.6 = (f32[1536,128]{1,0:T(8,128)S(1)}, f32[1536,128]{1,0:T(8,128)S(1)}, u32[]{:S(2)}, u32[]{:S(2)}) collective-permute-start(f32[1536,128]{1,0:T(8,128)S(1)} %skeleton.1.own_ref), channel_id=1, source_target_pairs={{0,16},{8,24},{16,0},{24,8},{1,17},{9,25},{17,1},{25,9},{2,18},{10... | collective-permute-start | bytes 2359304 | tf_op jit(solution)/shard_map/ppermute | solution.py:425
  81.4 39.1 %collective-permute-start = (f32[1056,128]{1,0:T(8,128)S(1)}, f32[1056,128]{1,0:T(8,128)S(1)}, u32[]{:S(2)}, u32[]{:S(2)}) collective-permute-start(f32[1056,128]{1,0:T(8,128)S(1)} %get-tuple-element.12.packed_ref), channel_id=1, source_target_pairs={{0,4},{1,5},{2,6},{3,7},{4,0},{5,1},{6,2},{7,3},{8,12},{9,13},{10,... | collective-permute-start | bytes 1622024 | tf_op jit(solution)/shard_map/ppermute | solution.py:407
  90.2 63.3 %collective-permute-start.5 = (f32[1536,128]{1,0:T(8,128)S(1)}, f32[1536,128]{1,0:T(8,128)S(1)}, u32[]{:S(2)}, u32[]{:S(2)}) collective-permute-start(f32[1536,128]{1,0:T(8,128)S(1)} %skeleton.1.own_ref), channel_id=1, source_target_pairs={{0,8},{8,0},{16,24},{24,16},{1,9},{9,1},{17,25},{25,17},{2,10},{10... | collective-permute-start | bytes 2359304 | tf_op jit(solution)/shard_map/ppermute | solution.py:425
  121.5 32.0 %collective-permute-start.7 = (f32[1536,128]{1,0:T(8,128)S(1)}, f32[1536,128]{1,0:T(8,128)S(1)}, u32[]{:S(2)}, u32[]{:S(2)}) collective-permute-start(f32[1536,128]{1,0:T(8,128)S(1)} %collective-permute-done.6.rest_1_), channel_id=1, source_target_pairs={{0,8},{8,0},{16,24},{24,16},{1,9},{9,1},{17,25},{25,17},{2,10},{10... | collective-permute-start | bytes 2359304 | tf_op jit(solution)/shard_map/ppermute | solution.py:425
  131.3 31.9 %collective-permute-start.4 = (f32[1536,128]{1,0:T(8,128)S(1)}, f32[1536,128]{1,0:T(8,128)S(1)}, u32[]{:S(2)}, u32[]{:S(2)}) collective-permute-start(f32[1536,128]{1,0:T(8,128)S(1)} %slice.13), channel_id=1, source_target_pairs={{1,0},{3,1},{2,3},{0,2},{5,4},{7,5},{6,7},{4,6},{9,8},{11,9},{10,1... | collective-permute-start | bytes 2359304 | tf_op jit(solution)/shard_map/ppermute | solution.py:410
  135.6 27.6 %collective-permute-start.2 = (f32[1536,128]{1,0:T(8,128)S(1)}, f32[1536,128]{1,0:T(8,128)S(1)}, u32[]{:S(2)}, u32[]{:S(2)}) collective-permute-start(f32[1536,128]{1,0:T(8,128)S(1)} %slice.12), channel_id=1, source_target_pairs={{0,1},{1,3},{3,2},{2,0},{4,5},{5,7},{7,6},{6,4},{8,9},{9,11},{11,1... | collective-permute-start | bytes 2359304 | tf_op jit(solution)/shard_map/ppermute | solution.py:409

commit v2 on v1

v2 whole, which is shorter than its diff:
```python
import functools
import math

import jax
import jax.numpy as jnp
from jax import lax
from jax.experimental import pallas as pl
from jax.experimental.pallas import tpu as pltpu
from jax.sharding import PartitionSpec as P


F32 = jnp.float32
BF16 = jnp.bfloat16
LANES = 128
JOINT = ("outer", "inner")
VMEM = pl.BlockSpec(memory_space=pltpu.VMEM)
SMEM = pl.BlockSpec(memory_space=pltpu.SMEM)
HBM = pl.BlockSpec(memory_space=pltpu.HBM)


def call(body, outs, args, in_specs, scratch=(), out_specs=None, flops=0):
    nbytes = sum(a.size * a.dtype.itemsize for a in (*args, *outs))
    held = sum(math.prod(s.shape) * jnp.dtype(s.dtype).itemsize for s in scratch if getattr(s, "memory_space", None) == pltpu.VMEM)
    limit = min(60 << 20, nbytes + held + (8 << 20))
    return pl.pallas_call(
        body,
        out_shape=outs,
        in_specs=in_specs,
        out_specs=out_specs or [VMEM] * len(outs),
        scratch_shapes=list(scratch),
        compiler_params=pltpu.CompilerParams(vmem_limit_bytes=limit),
        cost_estimate=pl.CostEstimate(flops=flops, bytes_accessed=nbytes, transcendentals=0),
    )(*args)


def split(x):
    hi = x.astype(BF16)
    return hi, (x - hi.astype(F32)).astype(BF16)


def pack(rows, dim):
    half = rows.shape[0] // 2
    return jnp.concatenate([rows[:half, :dim], rows[half:, :dim]], axis=1)


def exponent_side(packed, dim, scale, is_target):
    lane = lax.broadcasted_iota(jnp.int32, packed.shape, 1)
    first = lane < dim
    turned = jnp.concatenate([packed[:, dim:], packed[:, :dim]], axis=1)
    at = dim + (0 if is_target else 3)
    ones = jnp.where((lane >= dim) & (lane < dim + 6), 1.0, 0.0)
    blocks = []
    for x in (jnp.where(first, packed, turned), jnp.where(first, turned, packed)):
        n = jnp.sum(x * x, axis=1, keepdims=True) * (-0.5 * scale)
        norms = jnp.where(lane == at, n, ones)
        for j in (1, 2):
            n = n - n.astype(BF16).astype(F32)
            norms = jnp.where(lane == at + j, n, norms)
        if is_target:
            x = x * (2.0 * scale)
        low = x - x.astype(BF16).astype(F32)
        if is_target:
            head, tail = jnp.where(first, x, low), jnp.where(first, x, norms)
        else:
            head, tail = x, jnp.where(first, low, norms)
        blocks.append(jnp.concatenate([head, tail], axis=1).astype(BF16))
    return blocks


def load_points(ref, pitch, skip, base, out, scale, is_target):
    count = ref.shape[0] // pitch
    size = out.shape[1] // 2
    step = size
    parts = size // step

    def body(i, carry):
        g, c = div_mod(i, parts)
        at = pl.multiple_of(g * pitch + skip + c * step, 8)
        blocks = exponent_side(ref[pl.ds(at, step), :], LANES // 2, scale, is_target)
        for j, value in enumerate(blocks):
            out[base + g, pl.ds(pl.multiple_of(j * size + c * step, step), step), :] = value
        return carry

    lax.fori_loop(0, count * parts, body, 0)


def load_charges(ref, pitch, base, out):
    count = ref.shape[0] // pitch
    step = 256
    parts = out.shape[1] // step

    def body(i, carry):
        g, c = div_mod(i, parts)
        at = pl.multiple_of(g * pitch + c * step, 8)
        hi, lo = split(ref[pl.ds(at, step), :])
        rows = pl.ds(pl.multiple_of(c * step, step), step)
        out[base + g, rows, :LANES] = hi
        out[base + g, rows, LANES:] = lo
        return carry

    lax.fori_loop(0, count * parts, body, 0)


def charge_side(c):
    hi, lo = split(c)
    return jnp.concatenate([hi, lo], axis=1)


def nt_dot(a, b):
    return lax.dot_general(a, b, (((1,), (1,)), ((), ())), preferred_element_type=F32)


def tn_dot(a, b):
    return lax.dot_general(a, b, (((0,), (0,)), ((), ())), preferred_element_type=F32)


def fold(p):
    half = p.shape[1] // 2
    return p[:, :half] + p[:, half:]


def tile_product(target, source, charge):
    k = jnp.exp2(nt_dot(target, source))
    hi, lo = split(k)
    return fold(
        jnp.dot(hi, charge, preferred_element_type=F32)
        + jnp.dot(lo, charge, preferred_element_type=F32)
    )


def div_mod(x, n):
    if n & (n - 1) == 0:
        return lax.shift_right_logical(x, jnp.int32(n.bit_length() - 1)), x & (n - 1)
    q = lax.div(x, jnp.int32(n))
    return q, x - q * n


UNROLL = 64


def rows_loop(count, body):
    def step(i, carry):
        line, part = div_mod(i, LANES // UNROLL)
        for u in range(UNROLL):
            body(i * UNROLL + u, line, part * UNROLL + u)
        return carry

    lax.fori_loop(0, count // UNROLL, step, 0)


def send_kernel(devs, pair, block, order_hbm, pts_hbm, chg_hbm, send_ref, code_ref, ptmp, prow, order_ref, pts_ref, chg_ref, idx_v, idx_s, sem, sems):
    loads = [
        pltpu.make_async_copy(a, b, sems.at[i])
        for i, (a, b) in enumerate(((order_hbm, order_ref), (chg_hbm, chg_ref), (pts_hbm, pts_ref)))
    ]
    for load in loads:
        load.start()
    loads[0].wait()
    rows = chg_ref.shape[0]
    dim = pts_ref.shape[0]
    lines = rows // LANES
    dest, slot = div_mod(order_ref[...], rows)
    sub = lax.broadcasted_iota(jnp.int32, (devs, LANES), 0)
    hot = [jnp.where(dest[r : r + 1, :] == sub, 1.0, 0.0) for r in range(lines)]
    ki = lax.broadcasted_iota(jnp.int32, (LANES, 2 * LANES), 0)
    ji = lax.broadcasted_iota(jnp.int32, (LANES, 2 * LANES), 1)
    tri = jnp.where((ki < ji) | (ji >= LANES), 1.0, 0.0).astype(BF16)
    pre = jnp.dot(jnp.concatenate([h.astype(BF16) for h in hot], axis=0), tri, preferred_element_type=F32)
    base = jnp.zeros((devs, LANES), F32)
    ranks = []
    for r in range(lines):
        part = pre[r * devs : (r + 1) * devs]
        ranks.append(jnp.sum(hot[r] * (part[:, :LANES] + base), axis=0, keepdims=True))
        base = base + part[:, LANES:]
    rank_f = jnp.concatenate(ranks, axis=0)
    rank = rank_f.astype(jnp.int32)
    idx_v[...] = dest * block + rank
    copy = pltpu.make_async_copy(idx_v, idx_s, sem)
    copy.start()
    code_ref[...] = dest * pair + rank
    psub = lax.broadcasted_iota(jnp.int32, (pair, LANES), 0)
    s_hi = lax.shift_right_logical(slot, 8).astype(F32)
    s_lo = (slot & 255).astype(F32)
    left, right = [], []
    for r in range(lines):
        left.append(
            jnp.concatenate([hot[r] * s_hi[r : r + 1, :], hot[r] * s_lo[r : r + 1, :]], axis=0).astype(BF16)
        )
        right.append(jnp.where(rank[r : r + 1, :] == psub, 1.0, 0.0).astype(BF16))
    both = nt_dot(jnp.concatenate(left, axis=1), jnp.concatenate(right, axis=1))
    table = both[:devs] * 256.0 + both[devs:]
    if pair < LANES:
        table = jnp.concatenate([table, jnp.zeros((devs, LANES - pair), F32)], axis=1)
    loads[2].wait()
    for c in range(0, rows, 256):
        prow[c : c + 256, :dim] = pts_ref[:, c : c + 256].T
    loads[1].wait()
    copy.wait()

    def move(n, line, lane):
        j = idx_s[line, lane]
        send_ref[pl.ds(j, 1), :] = chg_ref[pl.ds(n, 1), :]
        ptmp[pl.ds(j, 1), :] = prow[pl.ds(n, 1), :]

    rows_loop(rows, move)
    half = pair // 2
    for d in range(devs):
        send_ref[d * block + pair : d * block + pair + half, :] = pack(
            ptmp[d * block : d * block + pair, :], dim
        )
        send_ref[d * block + pair + half : (d + 1) * block, :] = jnp.broadcast_to(
            table[d : d + 1, :], (block - pair - half, LANES)
        )


def place_kernel(devs, pair, block, leaf, dim, recv_ref, low_ref, high_ref, pts_ref, exch_ref, pos_ref, rolled, chg, pos_s, sem):
    half = pair // 2
    rows = pts_ref.shape[0]
    leaves = rows // leaf
    line = leaf + leaf // 2
    table = jnp.concatenate(
        [recv_ref[d * block + pair + half : d * block + pair + half + 1, :] for d in range(devs)], axis=0
    )
    pos_ref[...] = table.astype(jnp.int32)
    copy = pltpu.make_async_copy(pos_ref, pos_s, sem)
    copy.start()
    exch_ref[rows // 2 :, :] = table
    for d in range(devs):
        part = recv_ref[d * block + pair : d * block + pair + half, :]
        rolled[d * half : (d + 1) * half, :] = jnp.concatenate([part[:, dim:], part[:, :dim]], axis=1)
    copy.wait()

    def per_source(d, carry):
        for j in range(pair):
            p = pos_s[d, j]
            chg[pl.ds(p, 1), :] = recv_ref[pl.ds(d * block + j, 1), :]
            if j < half:
                pts_ref[pl.ds(p, 1), :] = recv_ref[pl.ds(d * block + pair + j, 1), :]
            else:
                pts_ref[pl.ds(p, 1), :] = rolled[pl.ds(d * half + j - half, 1), :]
        return carry

    lax.fori_loop(0, devs, per_source, 0)
    for g in range(leaves):
        packed = pack(pts_ref[g * leaf : (g + 1) * leaf, :], dim)
        ref, at = (low_ref, g * line) if g < leaves // 2 else (high_ref, (g - leaves // 2) * line)
        ref[at : at + leaf, :] = chg[g * leaf : (g + 1) * leaf, :]
        ref[at + leaf : at + line, :] = packed
        exch_ref[g * (leaf // 2) : (g + 1) * (leaf // 2), :] = packed


def skeleton_kernel(leaf, dim, low_ref, high_ref, pts_ref, interp_ref, skel_ref, far_ref, stmp):
    leaves, skel = skel_ref.shape
    line = leaf + leaf // 2
    fline = skel + skel // 2

    for g in range(leaves):

        def move(n, line, lane, g=g):
            stmp[pl.ds(g * skel + n, 1), :] = pts_ref[pl.ds(g * leaf + skel_ref[g, n], 1), :]

        rows_loop(skel, move)
    for g in range(leaves):
        hi, lo = split(interp_ref[g * leaf : (g + 1) * leaf, :])
        ref, at = (low_ref, g * line) if g < leaves // 2 else (high_ref, (g - leaves // 2) * line)
        charge = charge_side(ref[at : at + leaf, :])
        far_ref[g * fline : g * fline + skel, :] = fold(tn_dot(hi, charge) + tn_dot(lo, charge))
        far_ref[g * fline + skel : (g + 1) * fline, :] = pack(stmp[g * skel : (g + 1) * skel, :], dim)


def far_kernel(skel, scale, n_inner, blocks, far_rows_ref, own_ref, interp_ref, *rest):
    refs, (out_ref, src, chg, tgt) = rest[:blocks], rest[blocks:]
    leaves, fars = far_rows_ref.shape
    leaf = interp_ref.shape[0] // leaves
    fline = skel + skel // 2
    outer = lax.axis_index("outer")
    for b in range(blocks):
        load_points(refs[b], fline, skel, b * leaves, src, scale, False)
        load_charges(refs[b], fline, b * leaves, chg)
    load_points(own_ref, fline, skel, 0, tgt, scale, True)

    for g in range(leaves):
        q = jnp.zeros((skel, LANES), F32)
        for k in range(fars):
            device, local = div_mod(far_rows_ref[g, k], leaves)
            at = ((device // n_inner) ^ outer) * leaves - leaves + local
            q = q + tile_product(tgt[g], src[at], chg[at])
        qq = charge_side(q)
        hi, lo = split(interp_ref[g * leaf : (g + 1) * leaf, :])
        out_ref[g * leaf : (g + 1) * leaf, :] = fold(
            jnp.dot(hi, qq, preferred_element_type=F32) + jnp.dot(lo, qq, preferred_element_type=F32)
        )


def ring_place(member, bits):
    place, shift = member, 1
    while shift < bits:
        place = place ^ lax.shift_right_logical(member, jnp.int32(shift))
        shift += 1
    return place


def target_kernel(leaf, scale, own_ref, theirs_ref, out_ref):
    leaves = out_ref.shape[0] // 2
    for j, ref in enumerate((own_ref, theirs_ref)):
        load_points(ref.at[: leaves * leaf // 2], leaf // 2, 0, j * leaves, out_ref, scale, True)


CODE = 1024
GROUP = 2


def list_kernel(leaves, n_inner, near_ref, list_ref, count_ref):
    half = n_inner // 2
    n_near = near_ref.shape[1]
    bits = half.bit_length() - 1
    inner = lax.axis_index("inner")
    mine = ring_place(inner & (half - 1), bits)
    count_ref[0] = 0
    count_ref[1] = 0

    def add(row, code):
        n = count_ref[row]
        list_ref[row, n] = code
        count_ref[row] = n + 1

    def entry(e, carry):
        row, k = div_mod(e, n_near)
        device, local = div_mod(near_ref[row, k], leaves)
        member = device & (n_inner - 1)
        same_half = (member ^ inner) < half
        offset = (ring_place(member & (half - 1), bits) - mine) & (half - 1)
        slot = jnp.where(offset > half // 2, 2 * (half - offset) - 1, 2 * offset)

        @pl.when(same_half & (offset == half // 2))
        def _():
            add(1, row * CODE + local)

        @pl.when(same_half & (offset != half // 2) & ((member != inner) | (row >= leaves)))
        def _():
            add(0, row * CODE + slot * leaves + local)

        return carry

    lax.fori_loop(0, 2 * leaves * n_near, entry, 0)
    for row in range(2):
        for _ in range(GROUP - 1):

            @pl.when(count_ref[row] % GROUP != 0)
            def _():
                add(row, 2 * leaves * CODE)


def load_sources(leaf, scale, refs, src, chg):
    line = leaf + leaf // 2
    at = 0
    for ref in refs:
        load_points(ref, line, leaf, at, src, scale, False)
        load_charges(ref, line, at, chg)
        at += ref.shape[0] // line


def leaf_rows(t, c, leaf, step):
    return pl.ds(pl.multiple_of(t * leaf + c, step), step)


def self_kernel(leaf, scale, own_ref, low_ref, high_ref, acc_ref, src, chg, tgt):
    leaves = src.shape[0]
    load_sources(leaf, scale, (low_ref, high_ref), src, chg)
    load_points(own_ref.at[: leaves * leaf // 2], leaf // 2, 0, 0, tgt, scale, True)
    step = leaf // 2

    def entry(t, carry):
        for c in range(0, leaf, step):
            acc_ref[leaf_rows(t, c, leaf, step), :] = tile_product(
                tgt[t, c : c + step, :], src[t], chg[t]
            )
        return carry

    lax.fori_loop(0, leaves, entry, 0)


def add_listed(leaf, row, list_ref, count_ref, tgt, src, chg, acc):
    step = leaf // 2

    def entry(e, carry):
        for u in range(GROUP):
            t, at = div_mod(list_ref[row, e * GROUP + u], CODE)
            x = jnp.minimum(t, tgt.shape[0] - 1)
            for c in range(0, leaf, step):
                acc[leaf_rows(t, c, leaf, step), :] += tile_product(
                    tgt[x, c : c + step, :], src[at], chg[at]
                )
        return carry

    lax.fori_loop(0, lax.shift_right_logical(count_ref[row], jnp.int32(GROUP.bit_length() - 1)), entry, 0)


def near_kernel(leaf, scale, list_ref, count_ref, tgt_ref, *rest):
    *sources, acc_ref, src, chg = rest
    load_sources(leaf, scale, sources, src, chg)
    acc_ref[...] = jnp.zeros_like(acc_ref)
    add_listed(leaf, 0, list_ref, count_ref, tgt_ref, src, chg, acc_ref)


def last_kernel(devs, pair, leaf, scale, list_ref, count_ref, pos_ref, tgt_ref, low_ref, high_ref, old_ref, self_ref, far_ref, other_ref, out_ref, acc, src, chg, opos_v, opos_s, sem):
    rows = far_ref.shape[0]
    opos_v[...] = other_ref[...].astype(jnp.int32)
    copy = pltpu.make_async_copy(opos_v, opos_s, sem)
    copy.start()
    load_sources(leaf, scale, (low_ref, high_ref), src, chg)
    acc[:rows, :] = old_ref[:rows, :] + (self_ref[...] + far_ref[...])
    acc[rows:, :] = old_ref[rows:, :]
    add_listed(leaf, 1, list_ref, count_ref, tgt_ref, src, chg, acc)
    copy.wait()

    def per_source(d, carry):
        for j in range(pair):
            out_ref[pl.ds(d * 2 * pair + j, 1), :] = acc[pl.ds(pos_ref[d, j], 1), :]
            out_ref[pl.ds(d * 2 * pair + pair + j, 1), :] = acc[pl.ds(rows + opos_s[d, j], 1), :]
        return carry

    lax.fori_loop(0, devs, per_source, 0)


def final_kernel(pair, n_inner, ret_ref, code_ref, out_ref, both):
    devs = both.shape[0] // pair
    for d in range(devs):
        other = d ^ (n_inner // 2)
        both[d * pair : (d + 1) * pair, :] = (
            ret_ref[2 * d * pair : (2 * d + 1) * pair, :]
            + ret_ref[(2 * other + 1) * pair : (2 * other + 2) * pair, :]
        )

    def move(n, line, lane):
        out_ref[pl.ds(n, 1), :] = both[pl.ds(code_ref[line, lane], 1), :]

    rows_loop(out_ref.shape[0], move)


def shards(points, charges, interp, order, near, far, skel):
    n_inner = lax.axis_size("inner")
    n_outer = lax.axis_size("outer")
    devs = n_inner * n_outer
    rows, dim = points.shape
    leaves, n_skel = skel.shape
    leaf = rows // leaves
    line = leaf + leaf // 2
    fline = n_skel + n_skel // 2
    pair = rows // devs
    block = pair + pair // 2 + 8
    scale = (4.0 / dim) * math.log2(math.e)
    outer = lax.axis_index("outer")
    inner = lax.axis_index("inner")
    me = outer * n_inner + inner
    half = n_inner // 2
    partner = outer * n_inner + (inner ^ half)

    def f32(*shape):
        return jax.ShapeDtypeStruct(shape, F32)

    def i32(*shape):
        return jax.ShapeDtypeStruct(shape, jnp.int32)

    def near_of(device):
        return lax.dynamic_slice_in_dim(near, device * leaves, leaves, 0)

    near_rows = jnp.concatenate([near_of(me), near_of(partner)], axis=0)
    far_rows = lax.dynamic_slice_in_dim(far, me * leaves, leaves, 0)

    send, code = call(
        functools.partial(send_kernel, devs, pair, block),
        [f32(devs * block, LANES), i32(rows // LANES, LANES)],
        (order.reshape(rows // LANES, LANES), points.T, charges),
        [HBM] * 3,
        [
            pltpu.VMEM((devs * block, LANES), F32),
            pltpu.VMEM((rows, LANES), F32),
            pltpu.VMEM((rows // LANES, LANES), jnp.int32),
            pltpu.VMEM((dim, rows), F32),
            pltpu.VMEM((rows, LANES), F32),
            pltpu.VMEM((rows // LANES, LANES), jnp.int32),
            pltpu.SMEM((rows // LANES, LANES), jnp.int32),
            pltpu.SemaphoreType.DMA,
            pltpu.SemaphoreType.DMA((3,)),
        ],
    )
    recv = lax.all_to_all(send.reshape(devs, block, LANES), JOINT, 0, 0, tiled=True)
    piece = leaves // 2 * line
    own_low, own_high, pts, exch, pos = call(
        functools.partial(place_kernel, devs, pair, block, leaf, dim),
        [f32(piece, LANES), f32(piece, LANES), f32(rows, LANES), f32(rows // 2 + devs, LANES), i32(devs, LANES)],
        (recv.reshape(devs * block, LANES),),
        [VMEM],
        [
            pltpu.VMEM((devs * pair // 2, LANES), F32),
            pltpu.VMEM((rows, LANES), F32),
            pltpu.SMEM((devs, LANES), jnp.int32),
            pltpu.SemaphoreType.DMA,
        ],
    )

    loop = [j ^ (j >> 1) for j in range(half)]
    right = [
        (base + loop[j], base + loop[(j + 1) % half]) for base in (0, half) for j in range(half)
    ]
    left = [(b, a) for a, b in right]

    def shift(x, perm):
        return lax.ppermute(x, "inner", perm)

    blocks = {0: (own_low, own_high)}
    to_right = to_left = (own_low, own_high)
    for step in range(1, half // 2):
        ra = shift(to_right[0], right)
        lb = shift(to_left[1], left)
        rb = shift(to_right[1], right)
        la = shift(to_left[0], left)
        to_right, to_left = (ra, rb), (la, lb)
        blocks[half - step], blocks[step] = to_right, to_left
    theirs = shift(exch, [(i, i ^ half) for i in range(n_inner)])
    blocks[half // 2] = (shift(to_right[0], right), shift(to_left[1], left))

    (far_own,) = call(
        functools.partial(skeleton_kernel, leaf, dim),
        [f32(leaves * fline, LANES)],
        (own_low, own_high, pts, interp, skel),
        [VMEM, VMEM, VMEM, VMEM, SMEM],
        [pltpu.VMEM((leaves * n_skel, LANES), F32)],
        flops=2 * rows * n_skel * 3 * 128,
    )
    held = {0: far_own}
    bit = n_outer // 2
    while bit:
        perm = [(o, o ^ bit) for o in range(n_outer)]
        got = {}
        for r, v in held.items():
            got[r ^ bit] = lax.ppermute(v, "outer", perm)
        held.update(got)
        bit //= 2

    lists, counts = call(
        functools.partial(list_kernel, leaves, n_inner),
        [i32(2, 2 * leaves * near.shape[1]), i32(2)],
        (near_rows,),
        [SMEM],
        out_specs=[SMEM, SMEM],
    )

    def tiles(count):
        return [
            pltpu.VMEM((count, leaf, 4 * dim), BF16),
            pltpu.VMEM((count, leaf, 2 * LANES), BF16),
        ]

    per_leaf = 2 * leaf * leaf * 256 * 3
    (own_sum,) = call(
        functools.partial(self_kernel, leaf, scale),
        [f32(rows, LANES)],
        (exch, own_low, own_high),
        [VMEM] * 3,
        tiles(leaves) + tiles(leaves)[:1],
        flops=leaves * per_leaf,
    )
    (targets,) = call(
        functools.partial(target_kernel, leaf, scale),
        [jax.ShapeDtypeStruct((2 * leaves, leaf, 4 * dim), BF16)],
        (exch, theirs),
        [VMEM] * 2,
        flops=1 << 20,
    )
    early = [0] + [j for step in range(1, half // 2) for j in (half - step, step)]
    sources = [piece for j in early for piece in blocks[j]]
    (acc,) = call(
        functools.partial(near_kernel, leaf, scale),
        [f32(2 * rows + leaf, LANES)],
        (lists, counts, targets, *sources),
        [SMEM, SMEM] + [VMEM] * (1 + len(sources)),
        tiles(len(early) * leaves),
        flops=len(early) * 2 * leaves * per_leaf,
    )
    others = [held[r] for r in range(1, n_outer)]
    n_blocks = len(others) * leaves
    (far_part,) = call(
        functools.partial(far_kernel, n_skel, scale, n_inner, len(others)),
        [f32(rows, LANES)],
        (far_rows, far_own, interp, *others),
        [SMEM] + [VMEM] * (2 + len(others)),
        [
            pltpu.VMEM((n_blocks, n_skel, 4 * dim), BF16),
            pltpu.VMEM((n_blocks, n_skel, 2 * LANES), BF16),
            pltpu.VMEM((leaves, n_skel, 4 * dim), BF16),
        ],
        flops=leaves * 8 * 2 * n_skel * n_skel * 256 * 3,
    )
    (out,) = call(
        functools.partial(last_kernel, devs, pair, leaf, scale),
        [f32(devs * 2 * pair, LANES)],
        (lists, counts, pos, targets, *blocks[half // 2], acc, own_sum, far_part, theirs[rows // 2 :]),
        [SMEM] * 3 + [VMEM] * 7,
        [pltpu.VMEM((2 * rows + leaf, LANES), F32)]
        + tiles(leaves)
        + [
            pltpu.VMEM((devs, LANES), jnp.int32),
            pltpu.SMEM((devs, LANES), jnp.int32),
            pltpu.SemaphoreType.DMA,
        ],
        flops=2 * leaves * per_leaf,
    )
    returned = lax.all_to_all(out.reshape(devs, 2 * pair, LANES), JOINT, 0, 0, tiled=True)
    (final,) = call(
        functools.partial(final_kernel, pair, n_inner),
        [f32(rows, LANES)],
        (returned.reshape(devs * 2 * pair, LANES), code),
        [VMEM, SMEM],
        [pltpu.VMEM((rows, LANES), F32)],
    )
    return final


def solution(mesh):
    row = P(JOINT, None)
    in_specs = (row, row, row, P(JOINT), P(), P(), row)
    return jax.shard_map(shards, mesh=mesh, in_specs=in_specs, out_specs=row, check_vma=False)
```

time: 249 us -> 216 us (0.87)
  Pallas kernels: 96.9 us -> 68.9 us
  between operations: 6.68 us -> 0.22 us
    pallas_call x12 -> x10, Pallas kernels: 96.9 us -> 68.9 us  [call(): pl.pallas_call(body, out_shape=outs, in_specs=in_specs, out_specs=out_spe...]
    ppermute x8 -> x10, waiting for transfers between devices: 29.4 us -> 30.8 us  [the longest x7 30.8 us: shift(): return lax.ppermute(x, 'inner', perm)]
    ppermute x8 -> x10, starting transfers between devices: 6.56 us -> 6.85 us  [the longest x7 5.7 us: shift(): return lax.ppermute(x, 'inner', perm)]
  transfers between devices with their start and end apart: 8 -> 10, of which waited for: 1 -> 2; matrix products, arithmetic and copies ran while one was open for 2% -> 0% of each run, Pallas kernels for 17% -> 20%
where the time goes in v2:
time: 216 us; the launch traced here: 215 us
  blocking collectives  104 us (48%)
  Pallas kernels  68.9 us (32%)
  waiting for transfers between devices  30.8 us (14%)
  starting transfers between devices  6.85 us (3%)
  local copies, waits for them, and re-layouts  4.44 us (2%)
    pallas_call x10, Pallas kernels, call(): pl.pallas_call(body, out_shape=outs, in_specs=in_specs, out_specs=out_spe...  68.9 us
    all_to_all x1, blocking collectives, shards(): lax.all_to_all(out.reshape(devs, 2 * pair, LANES), JOINT, 0, 0, tiled=True)  55.3 us
    all_to_all x1, blocking collectives, shards(): lax.all_to_all(send.reshape(devs, block, LANES), JOINT, 0, 0, tiled=True)  48.6 us
    ppermute x7, waiting for transfers between devices, shift(): return lax.ppermute(x, 'inner', perm)  30.8 us
    ppermute x7, starting transfers between devices, shift(): return lax.ppermute(x, 'inner', perm)  5.7 us
  transfers between devices with their start and end apart: 10, of which 2 were waited for; matrix products, arithmetic and copies ran while one was open for 0% of the time, Pallas kernels for 20%

profile of v2, /device:TPU:0, one launch (start us, length us, event | category | flops | bytes accessed | tf_op | source)
XLA Modules:
  0.0 215.3 jit_solution(5426445594335564364)
XLA Ops:
  0.0 1.2 copy-done.2
  1.2 1.0 copy-done.5
  2.3 0.7 copy-done.6
  3.0 6.3 %shard_map.74 = (f32[3328,128]{1,0:T(8,128)S(1)}, s32[16,128]{1,0:T(8,128)S(1)}) custom-call(s32[16,128]{1,0:T(8,128)S(1)} %bitcast.11, f32[64,2048]{1,0:T(8,128)S(1)} %bitcast.10, f32[2048,128]{1,0:T(8,128)S(1)} %copy-done.2), custom_call_target="tpu_custom_call" | custom-call | bytes 3293184 | tf_op jit(solution)/shard_map/pallas_call | solution.py:25
  9.4 48.6 %all_to_all.10 = f32[32,104,128]{2,1,0:T(8,128)S(1)} all-to-all(f32[32,104,128]{2,1,0:T(8,128)S(1)} %bitcast.9), channel_id=1, replica_groups=mesh['outer'=4,'inner'=8] {'outer','inner'}, dimensions={0} | all-to-all | bytes 3407872 | tf_op jit(solution)/shard_map/all_to_all | solution.py:488
  58.0 4.6 %shard_map.75 = (f32[1536,128]{1,0:T(8,128)}, f32[1536,128]{1,0:T(8,128)}, f32[2048,128]{1,0:T(8,128)S(1)}, f32[1056,128]{1,0:T(8,128)S(1)}, s32[32,128]{1,0:T(8,128)S(1)}) custom-call(f32[3328,128]{1,0:T(8,128)S(1)} %bitcast.7), custom_call_target="tpu_custom_call" | custom-call | bytes 4882432 | tf_op jit(solution)/shard_map/pallas_call | solution.py:25
  62.7 4.5 %shard_map.79.own_ref = f32[1536,128]{1,0:T(8,128)S(1)} custom-call(f32[1536,128]{1,0:T(8,128)} %get-tuple-element.19.rest_0_.low_ref, f32[1536,128]{1,0:T(8,128)} %get-tuple-element.20.rest_1_.high_ref, f32[2048,128]{1,0:T(8,128)S(1)} %get-tuple-element.21.pts_ref, f32[2048,256]{1,0:T(8,128)S(1)} %copy-done.1, s32[4,256]{1,0:T(4,128)S(1)} %copy-done.7), custom_call_target="tpu_custom_call" | custom-call | flops 402653184 | bytes 5509120 | tf_op jit(solution)/shard_map/pallas_call | solution.py:25
  67.2 0.6 collective-permute-start.8
  67.8 1.6 collective-permute-start.1
  69.4 0.9 collective-permute-start.3
  70.3 1.1 collective-permute-start.5
  71.4 17.8 %collective-permute-done.theirs_ref = f32[1056,128]{1,0:T(8,128)S(1)} collective-permute-done((f32[1056,128]{1,0:T(8,128)S(1)}, f32[1056,128]{1,0:T(8,128)S(1)}, u32[]{:S(2)}, u32[]{:S(2)}) %collective-permute-start) | collective-permute-done | bytes 540704 | tf_op jit(solution)/shard_map/ppermute | solution.py:510
  89.6 2.3 %shard_map.73 = (s32[2,64]{1,0:T(2,128)S(1)}, s32[2]{0:T(128)S(1)}) custom-call(s32[8,8]{1,0:T(8,128)S(1)} %pad_add_fusion.near_ref), custom_call_target="tpu_custom_call" | custom-call | bytes 776 | tf_op jit(solution)/shard_map/pallas_call | solution.py:25
  92.0 1.0 copy-done.4
  93.0 6.1 %shard_map.78.self_ref = f32[2048,128]{1,0:T(8,128)S(1)} custom-call(f32[1056,128]{1,0:T(8,128)S(1)} %copy-done.4, f32[1536,128]{1,0:T(8,128)} %get-tuple-element.19.rest_0_.low_ref, f32[1536,128]{1,0:T(8,128)} %get-tuple-element.20.rest_1_.high_ref), custom_call_target="tpu_custom_call" | custom-call | flops 1610612736 | bytes 3162112 | tf_op jit(solution)/shard_map/pallas_call | solution.py:25
  99.1 2.1 shard_map.76.tgt_ref
  101.3 0.5 collective-permute-start.9
  101.8 2.0 collective-permute-start.2
  103.8 13.0 %collective-permute-done.5.rest_3_ = f32[1536,128]{1,0:T(8,128)} collective-permute-done((f32[1536,128]{1,0:T(8,128)}, f32[1536,128]{1,0:T(8,128)}, u32[]{:S(2)}, u32[]{:S(2)}) %collective-permute-start.5) | collective-permute-done | bytes 786464 | tf_op jit(solution)/shard_map/ppermute | solution.py:510
  116.8 16.6 %shard_map.77.old_ref = f32[4608,128]{1,0:T(8,128)S(1)} custom-call(s32[2,64]{1,0:T(2,128)S(1)} %get-tuple-element.14.list_ref, s32[2]{0:T(128)S(1)} %get-tuple-element.15.count_ref, bf16[8,512,256]{2,1,0:T(8,128)(2,1)S(1)} %shard_map.76.tgt_ref, f32[1536,128]{1,0:T(8,128)} %get-tuple-element.19.rest_0_.low_ref, ...), custom_call_target="tpu_custom_call" | custom-call | flops 9663676416 | bytes 9175560 | tf_op jit(solution)/shard_map/pallas_call | solution.py:25
  133.5 10.9 %shard_map.80.far_ref = f32[2048,128]{1,0:T(8,128)S(1)} custom-call(s32[4,8]{1,0:T(4,128)S(1)} %copy.13.far_rows_ref, f32[1536,128]{1,0:T(8,128)S(1)} %shard_map.79.own_ref, f32[2048,256]{1,0:T(8,128)S(1)} %copy-done.1, f32[1536,128]{1,0:T(8,128)S(1)} %collective-permute-done.7.rest_0_, f32[1536,128]{1,0:T(8,128)} %collective-permute-done.8.rest_1_, ...), custom_call_target="tpu_custom_call" | custom-call | flops 3221225472 | bytes 6291584 | tf_op jit(solution)/shard_map/pallas_call | solution.py:25
  144.5 9.2 %shard_map.81 = f32[4096,128]{1,0:T(8,128)S(1)} custom-call(s32[2,64]{1,0:T(2,128)S(1)} %get-tuple-element.14.list_ref, s32[2]{0:T(128)S(1)} %get-tuple-element.15.count_ref, s32[32,128]{1,0:T(8,128)S(1)} %get-tuple-element.17.pos_ref, bf16[8,512,256]{2,1,0:T(8,128)(2,1)S(1)} %shard_map.76.tgt_ref, f32[1536,128]{1,0:T(8,128)S(1)} %collective-permute-done.2.low_ref, ...), custom_call_target="tpu_custom_call" | custom-call | flops 3221225472 | bytes 10256904 | tf_op jit(solution)/shard_map/pallas_call | solution.py:25
  153.7 55.3 %all_to_all.11 = f32[32,128,128]{2,1,0:T(8,128)S(1)} all-to-all(f32[32,128,128]{2,1,0:T(8,128)S(1)} %bitcast.8), channel_id=1, replica_groups=mesh['outer'=4,'inner'=8] {'outer','inner'}, dimensions={0} | all-to-all | bytes 4194304 | tf_op jit(solution)/shard_map/all_to_all | solution.py:610
  209.0 6.2 %shard_map.82 = f32[2048,128]{1,0:T(8,128)} custom-call(f32[4096,128]{1,0:T(8,128)S(1)} %bitcast.6, s32[16,128]{1,0:T(8,128)S(1)} %get-tuple-element.22.code_ref), custom_call_target="tpu_custom_call" | custom-call | bytes 3153920 | tf_op jit(solution)/shard_map/pallas_call | solution.py:25
  (33 shorter events, 0.6 us)
Async XLA Ops:
  0.0 89.2 %copy-start = (s32[128,8]{0,1:T(8,128)S(1)}, s32[128,8]{0,1:T(8,128)}, u32[]{:S(2)}) copy-start(s32[128,8]{0,1:T(8,128)} %param.12) | copy-start | bytes 12292
  0.0 1.2 copy-start.2
  1.2 1.0 copy-start.5
  2.3 0.7 copy-start.6
  9.3 53.4 %copy-start.1 = (f32[2048,256]{1,0:T(8,128)S(1)}, f32[2048,256]{1,0:T(8,128)}, u32[]{:S(2)}) copy-start(f32[2048,256]{1,0:T(8,128)} %interp_ref.3) | copy-start | bytes 6291460
  9.3 53.4 %copy-start.7 = (s32[4,256]{1,0:T(4,128)S(1)}, s32[4,256]{1,0:T(4,128)}, u32[]{:S(2)}) copy-start(s32[4,256]{1,0:T(4,128)} %skel_ref.1) | copy-start | bytes 12292
  62.6 4.6 %copy-start.3 = (f32[1056,128]{1,0:T(8,128)}, f32[1056,128]{1,0:T(8,128)S(1)}, u32[]{:S(2)}) copy-start(f32[1056,128]{1,0:T(8,128)S(1)} %get-tuple-element.18.own_ref) | copy-start | bytes 1622020
  62.6 26.6 %collective-permute-start = (f32[1056,128]{1,0:T(8,128)S(1)}, f32[1056,128]{1,0:T(8,128)S(1)}, u32[]{:S(2)}, u32[]{:S(2)}) collective-permute-start(f32[1056,128]{1,0:T(8,128)S(1)} %get-tuple-element.18.own_ref), channel_id=1, source_target_pairs={{0,4},{1,5},{2,6},{3,7},{4,0},{5,1},{6,2},{7,3},{8,12},{9,13},{10,... | collective-permute-start | bytes 1622024 | tf_op jit(solution)/shard_map/ppermute | solution.py:510
  62.7 26.6 %copy-start.8 = (s32[128,8]{0,1:T(8,128)S(1)}, s32[128,8]{0,1:T(8,128)}, u32[]{:S(2)}) copy-start(s32[128,8]{0,1:T(8,128)} %param.11) | copy-start | bytes 12292
  67.2 34.0 %collective-permute-start.8 = (f32[1536,128]{1,0:T(8,128)S(1)}, f32[1536,128]{1,0:T(8,128)}, u32[]{:S(2)}, u32[]{:S(2)}) collective-permute-start(f32[1536,128]{1,0:T(8,128)S(1)} %shard_map.79.own_ref), channel_id=1, source_target_pairs={{0,16},{8,24},{16,0},{24,8},{1,17},{9,25},{17,1},{25,9},{2,18},{10... | collective-permute-start | bytes 2359304 | tf_op jit(solution)/shard_map/ppermute | solution.py:538
  67.8 33.5 %collective-permute-start.1 = (f32[1536,128]{1,0:T(8,128)}, f32[1536,128]{1,0:T(8,128)}, u32[]{:S(2)}, u32[]{:S(2)}) collective-permute-start(f32[1536,128]{1,0:T(8,128)} %get-tuple-element.19.rest_0_.low_ref), channel_id=1, source_target_pairs={{0,1},{1,3},{3,2},{2,0},{4,5},{5,7},{7,6},{6,4},{8,9},{9,11},{11,1... | collective-permute-start | bytes 2359304 | tf_op jit(solution)/shard_map/ppermute | solution.py:510
  69.4 32.5 %collective-permute-start.3 = (f32[1536,128]{1,0:T(8,128)}, f32[1536,128]{1,0:T(8,128)}, u32[]{:S(2)}, u32[]{:S(2)}) collective-permute-start(f32[1536,128]{1,0:T(8,128)} %get-tuple-element.20.rest_1_.high_ref), channel_id=1, source_target_pairs={{1,0},{3,1},{2,3},{0,2},{5,4},{7,5},{6,7},{4,6},{9,8},{11,9},{10,1... | collective-permute-start | bytes 2359304 | tf_op jit(solution)/shard_map/ppermute | solution.py:510
  70.3 46.6 %collective-permute-start.5 = (f32[1536,128]{1,0:T(8,128)}, f32[1536,128]{1,0:T(8,128)}, u32[]{:S(2)}, u32[]{:S(2)}) collective-permute-start(f32[1536,128]{1,0:T(8,128)} %get-tuple-element.20.rest_1_.high_ref), channel_id=1, source_target_pairs={{0,1},{1,3},{3,2},{2,0},{4,5},{5,7},{7,6},{6,4},{8,9},{9,11},{11,1... | collective-permute-start | bytes 2359304 | tf_op jit(solution)/shard_map/ppermute | solution.py:510
  89.2 27.6 %collective-permute-start.6 = (f32[1536,128]{1,0:T(8,128)}, f32[1536,128]{1,0:T(8,128)}, u32[]{:S(2)}, u32[]{:S(2)}) collective-permute-start(f32[1536,128]{1,0:T(8,128)} %get-tuple-element.19.rest_0_.low_ref), channel_id=1, source_target_pairs={{1,0},{3,1},{2,3},{0,2},{5,4},{7,5},{6,7},{4,6},{9,8},{11,9},{10,1... | collective-permute-start | bytes 2359304 | tf_op jit(solution)/shard_map/ppermute | solution.py:510
  92.0 1.0 copy-start.4
  101.2 32.2 %collective-permute-start.7 = (f32[1536,128]{1,0:T(8,128)S(1)}, f32[1536,128]{1,0:T(8,128)S(1)}, u32[]{:S(2)}, u32[]{:S(2)}) collective-permute-start(f32[1536,128]{1,0:T(8,128)S(1)} %shard_map.79.own_ref), channel_id=1, source_target_pairs={{0,8},{8,0},{16,24},{24,16},{1,9},{9,1},{17,25},{25,17},{2,10},{10... | collective-permute-start | bytes 2359304 | tf_op jit(solution)/shard_map/ppermute | solution.py:538
  101.3 32.2 %collective-permute-start.9 = (f32[1536,128]{1,0:T(8,128)}, f32[1536,128]{1,0:T(8,128)S(1)}, u32[]{:S(2)}, u32[]{:S(2)}) collective-permute-start(f32[1536,128]{1,0:T(8,128)} %collective-permute-done.8.rest_1_), channel_id=1, source_target_pairs={{0,8},{8,0},{16,24},{24,16},{1,9},{9,1},{17,25},{25,17},{2,10},{10... | collective-permute-start | bytes 2359304 | tf_op jit(solution)/shard_map/ppermute | solution.py:538
  101.8 42.6 %collective-permute-start.2 = (f32[1536,128]{1,0:T(8,128)}, f32[1536,128]{1,0:T(8,128)S(1)}, u32[]{:S(2)}, u32[]{:S(2)}) collective-permute-start(f32[1536,128]{1,0:T(8,128)} %collective-permute-done.1.rest_2_), channel_id=1, source_target_pairs={{0,1},{1,3},{3,2},{2,0},{4,5},{5,7},{7,6},{6,4},{8,9},{9,11},{11,1... | collective-permute-start | bytes 2359304 | tf_op jit(solution)/shard_map/ppermute | solution.py:510
  116.8 27.6 %collective-permute-start.4 = (f32[1536,128]{1,0:T(8,128)}, f32[1536,128]{1,0:T(8,128)S(1)}, u32[]{:S(2)}, u32[]{:S(2)}) collective-permute-start(f32[1536,128]{1,0:T(8,128)} %collective-permute-done.3.rest_5_), channel_id=1, source_target_pairs={{1,0},{3,1},{2,3},{0,2},{5,4},{7,5},{6,7},{4,6},{9,8},{11,9},{10,1... | collective-permute-start | bytes 2359304 | tf_op jit(solution)/shard_map/ppermute | solution.py:510

commit v3 on v2

--- a/solution.py
+++ b/solution.py
@@ -18,10 +18,10 @@
 HBM = pl.BlockSpec(memory_space=pltpu.HBM)
 
 
-def call(body, outs, args, in_specs, scratch=(), out_specs=None, flops=0):
+def call(body, outs, args, in_specs, scratch=(), out_specs=None, flops=0, room=3):
     nbytes = sum(a.size * a.dtype.itemsize for a in (*args, *outs))
     held = sum(math.prod(s.shape) * jnp.dtype(s.dtype).itemsize for s in scratch if getattr(s, "memory_space", None) == pltpu.VMEM)
-    limit = min(60 << 20, nbytes + held + (8 << 20))
+    limit = min(60 << 20, nbytes + held + (room << 20))
     return pl.pallas_call(
         body,
         out_shape=outs,
@@ -268,56 +268,58 @@
         far_ref[g * fline + skel : (g + 1) * fline, :] = pack(stmp[g * skel : (g + 1) * skel, :], dim)
 
 
-def far_kernel(skel, scale, n_inner, blocks, far_rows_ref, own_ref, interp_ref, *rest):
-    refs, (out_ref, src, chg, tgt) = rest[:blocks], rest[blocks:]
+def far_kernel(skel, scale, n_inner, blocks, far_rows_ref, own_hbm, interp_hbm, *rest):
+    hbm, (out_ref, src, chg, tgt), bufs, sems = rest[:blocks], rest[blocks : blocks + 4], rest[blocks + 4 : -1], rest[-1]
+    own, *refs, interp = bufs
+    copies = start_loads([own_hbm, *hbm, interp_hbm], bufs, sems)
     leaves, fars = far_rows_ref.shape
-    leaf = interp_ref.shape[0] // leaves
+    leaf = interp_hbm.shape[0] // leaves
     fline = skel + skel // 2
     outer = lax.axis_index("outer")
+    copies[0].wait()
+    load_points(own, fline, skel, 0, tgt, scale, True)
     for b in range(blocks):
+        copies[b + 1].wait()
         load_points(refs[b], fline, skel, b * leaves, src, scale, False)
         load_charges(refs[b], fline, b * leaves, chg)
-    load_points(own_ref, fline, skel, 0, tgt, scale, True)
+    copies[-1].wait()
 
     for g in range(leaves):
         q = jnp.zeros((skel, LANES), F32)
-        for k in range(fars):
-            device, local = div_mod(far_rows_ref[g, k], leaves)
-            at = ((device // n_inner) ^ outer) * leaves - leaves + local
-            q = q + tile_product(tgt[g], src[at], chg[at])
+        for k in range(0, fars, 2):
+            ats = []
+            for j in range(k, min(k + 2, fars)):
+                device, local = div_mod(far_rows_ref[g, j], leaves)
+                ats.append(((device // n_inner) ^ outer) * leaves - leaves + local)
+            q = q + tile_product(
+                tgt[g],
+                jnp.concatenate([src[at] for at in ats], axis=0),
+                jnp.concatenate([chg[at] for at in ats], axis=0),
+            )
         qq = charge_side(q)
-        hi, lo = split(interp_ref[g * leaf : (g + 1) * leaf, :])
+        hi, lo = split(interp[g * leaf : (g + 1) * leaf, :])
         out_ref[g * leaf : (g + 1) * leaf, :] = fold(
             jnp.dot(hi, qq, preferred_element_type=F32) + jnp.dot(lo, qq, preferred_element_type=F32)
         )
 
 
-def ring_place(member, bits):
-    place, shift = member, 1
-    while shift < bits:
-        place = place ^ lax.shift_right_logical(member, jnp.int32(shift))
-        shift += 1
-    return place
-
-
 def target_kernel(leaf, scale, own_ref, theirs_ref, out_ref):
-    leaves = out_ref.shape[0] // 2
-    for j, ref in enumerate((own_ref, theirs_ref)):
-        load_points(ref.at[: leaves * leaf // 2], leaf // 2, 0, j * leaves, out_ref, scale, True)
+    leaves = own_ref.shape[0]
+    out_ref[:leaves] = own_ref[...]
+    load_points(theirs_ref.at[: leaves * leaf // 2], leaf // 2, 0, leaves, out_ref, scale, True)
 
 
 CODE = 1024
-GROUP = 2
+GROUP = 4
 
 
 def list_kernel(leaves, n_inner, near_ref, list_ref, count_ref):
     half = n_inner // 2
+    cut = leaves // 2
     n_near = near_ref.shape[1]
-    bits = half.bit_length() - 1
     inner = lax.axis_index("inner")
-    mine = ring_place(inner & (half - 1), bits)
-    count_ref[0] = 0
-    count_ref[1] = 0
+    for row in range(4):
+        count_ref[row] = 0
 
     def add(row, code):
         n = count_ref[row]
@@ -327,34 +329,40 @@
     def entry(e, carry):
         row, k = div_mod(e, n_near)
         device, local = div_mod(near_ref[row, k], leaves)
-        member = device & (n_inner - 1)
-        same_half = (member ^ inner) < half
-        offset = (ring_place(member & (half - 1), bits) - mine) & (half - 1)
-        slot = jnp.where(offset > half // 2, 2 * (half - offset) - 1, 2 * offset)
-
-        @pl.when(same_half & (offset == half // 2))
+        away = (device & (n_inner - 1)) ^ inner
+        last = away == half - 1
+        high = local >= cut
+        theirs = row >= leaves
+        which = jnp.where(last, jnp.where(high, 3, 2), jnp.where(theirs, 1, 0))
+        source = jnp.where(last, jnp.where(high, local - cut, local), away * leaves + local)
+
+        @pl.when((away < half) & ((away != 0) | theirs))
         def _():
-            add(1, row * CODE + local)
-
-        @pl.when(same_half & (offset != half // 2) & ((member != inner) | (row >= leaves)))
-        def _():
-            add(0, row * CODE + slot * leaves + local)
+            add(which, row * CODE + source)
 
         return carry
 
     lax.fori_loop(0, 2 * leaves * n_near, entry, 0)
-    for row in range(2):
+    for row in range(4):
         for _ in range(GROUP - 1):
 
             @pl.when(count_ref[row] % GROUP != 0)
             def _():
-                add(row, 2 * leaves * CODE)
-
-
-def load_sources(leaf, scale, refs, src, chg):
+                add(row, (leaves if row == 0 else 2 * leaves) * CODE)
+
+
+def start_loads(hbm_refs, bufs, sems):
+    copies = [pltpu.make_async_copy(a, b, sems.at[i]) for i, (a, b) in enumerate(zip(hbm_refs, bufs))]
+    for copy in copies:
+        copy.start()
+    return copies
+
+
+def load_sources(leaf, scale, refs, src, chg, at=0, copies=None):
     line = leaf + leaf // 2
-    at = 0
-    for ref in refs:
+    for i, ref in enumerate(refs):
+        if copies:
+            copies[i].wait()
         load_points(ref, line, leaf, at, src, scale, False)
         load_charges(ref, line, at, chg)
         at += ref.shape[0] // line
@@ -370,14 +378,15 @@
     load_points(own_ref.at[: leaves * leaf // 2], leaf // 2, 0, 0, tgt, scale, True)
     step = leaf // 2
 
-    def entry(t, carry):
-        for c in range(0, leaf, step):
-            acc_ref[leaf_rows(t, c, leaf, step), :] = tile_product(
-                tgt[t, c : c + step, :], src[t], chg[t]
-            )
-        return carry
-
-    lax.fori_loop(0, leaves, entry, 0)
+    def entry(e, carry):
+        for t in (2 * e, 2 * e + 1):
+            for c in range(0, leaf, step):
+                acc_ref[leaf_rows(t, c, leaf, step), :] = tile_product(
+                    tgt[t, c : c + step, :], src[t], chg[t]
+                )
+        return carry
+
+    lax.fori_loop(0, leaves // 2, entry, 0)
 
 
 def add_listed(leaf, row, list_ref, count_ref, tgt, src, chg, acc):
@@ -396,22 +405,40 @@
     lax.fori_loop(0, lax.shift_right_logical(count_ref[row], jnp.int32(GROUP.bit_length() - 1)), entry, 0)
 
 
-def near_kernel(leaf, scale, list_ref, count_ref, tgt_ref, *rest):
-    *sources, acc_ref, src, chg = rest
-    load_sources(leaf, scale, sources, src, chg)
+def own_near_kernel(leaf, scale, list_ref, count_ref, tgt_ref, src_ref, chg_ref, *rest):
+    n = (len(rest) - 4) // 2
+    sources, (acc_ref, src, chg), bufs, sems = rest[:n], rest[n : n + 3], rest[n + 3 : -1], rest[-1]
+    copies = start_loads(sources, bufs, sems)
+    leaves = src_ref.shape[0]
+    src[:leaves] = src_ref[...]
+    chg[:leaves] = chg_ref[...]
     acc_ref[...] = jnp.zeros_like(acc_ref)
+    load_sources(leaf, scale, bufs, src, chg, leaves, copies)
     add_listed(leaf, 0, list_ref, count_ref, tgt_ref, src, chg, acc_ref)
 
 
-def last_kernel(devs, pair, leaf, scale, list_ref, count_ref, pos_ref, tgt_ref, low_ref, high_ref, old_ref, self_ref, far_ref, other_ref, out_ref, acc, src, chg, opos_v, opos_s, sem):
+def near_kernel(leaf, scale, list_ref, count_ref, tgt_ref, src_ref, chg_ref, low_hbm, own_ref, acc_ref, src, chg, low, sems):
+    rows = own_ref.shape[0] - leaf
+    copies = start_loads([low_hbm], [low], sems)
+    acc_ref[:rows, :] = own_ref[:rows, :]
+    acc_ref[rows:, :] = jnp.zeros((acc_ref.shape[0] - rows, LANES), F32)
+    add_listed(leaf, 1, list_ref, count_ref, tgt_ref, src_ref, chg_ref, acc_ref)
+    load_sources(leaf, scale, (low,), src, chg, 0, copies)
+    add_listed(leaf, 2, list_ref, count_ref, tgt_ref, src, chg, acc_ref)
+
+
+def last_kernel(devs, pair, leaf, scale, list_ref, count_ref, pos_ref, tgt_ref, piece_hbm, old_ref, self_ref, far_ref, theirs_hbm, out_ref, acc, src, chg, opos_v, opos_s, sem, held, opos_f, sems):
     rows = far_ref.shape[0]
-    opos_v[...] = other_ref[...].astype(jnp.int32)
+    table = theirs_hbm.at[pl.ds(rows // 2, devs), :]
+    copies = start_loads([piece_hbm, table], [held, opos_f], sems)
+    copies[1].wait()
+    opos_v[...] = opos_f[...].astype(jnp.int32)
     copy = pltpu.make_async_copy(opos_v, opos_s, sem)
     copy.start()
-    load_sources(leaf, scale, (low_ref, high_ref), src, chg)
     acc[:rows, :] = old_ref[:rows, :] + (self_ref[...] + far_ref[...])
     acc[rows:, :] = old_ref[rows:, :]
-    add_listed(leaf, 1, list_ref, count_ref, tgt_ref, src, chg, acc)
+    load_sources(leaf, scale, (held,), src, chg, 0, copies)
+    add_listed(leaf, 3, list_ref, count_ref, tgt_ref, src, chg, acc)
     copy.wait()
 
     def per_source(d, carry):
@@ -423,7 +450,7 @@
     lax.fori_loop(0, devs, per_source, 0)
 
 
-def final_kernel(pair, n_inner, ret_ref, code_ref, out_ref, both):
+def final_kernel(pair, n_inner, ret_ref, code_ref, out_hbm, both, out, sems):
     devs = both.shape[0] // pair
     for d in range(devs):
         other = d ^ (n_inner // 2)
@@ -432,10 +459,25 @@
             + ret_ref[(2 * other + 1) * pair : (2 * other + 2) * pair, :]
         )
 
-    def move(n, line, lane):
-        out_ref[pl.ds(n, 1), :] = both[pl.ds(code_ref[line, lane], 1), :]
-
-    rows_loop(out_ref.shape[0], move)
+    parts = sems.shape[0]
+    size = out.shape[0] // parts
+    steps = size // UNROLL
+    copies = []
+    for p in range(parts):
+
+        def step(i, carry):
+            line, part = div_mod(i, LANES // UNROLL)
+            for u in range(UNROLL):
+                row = both[pl.ds(code_ref[line, part * UNROLL + u], 1), :]
+                out[pl.ds(i * UNROLL + u, 1), :] = row
+            return carry
+
+        lax.fori_loop(p * steps, (p + 1) * steps, step, 0)
+        rows = pl.ds(p * size, size)
+        copies.append(pltpu.make_async_copy(out.at[rows, :], out_hbm.at[rows, :], sems.at[p]))
+        copies[-1].start()
+    for copy in copies:
+        copy.wait()
 
 
 def shards(points, charges, interp, order, near, far, skel):
@@ -484,6 +526,7 @@
             pltpu.SemaphoreType.DMA,
             pltpu.SemaphoreType.DMA((3,)),
         ],
+        room=60,
     )
     recv = lax.all_to_all(send.reshape(devs, block, LANES), JOINT, 0, 0, tiled=True)
     piece = leaves // 2 * line
@@ -500,26 +543,16 @@
         ],
     )
 
-    loop = [j ^ (j >> 1) for j in range(half)]
-    right = [
-        (base + loop[j], base + loop[(j + 1) % half]) for base in (0, half) for j in range(half)
-    ]
-    left = [(b, a) for a, b in right]
-
-    def shift(x, perm):
-        return lax.ppermute(x, "inner", perm)
+    def swap(x, bit):
+        return lax.ppermute(x, "inner", [(i, i ^ bit) for i in range(n_inner)])
 
     blocks = {0: (own_low, own_high)}
-    to_right = to_left = (own_low, own_high)
-    for step in range(1, half // 2):
-        ra = shift(to_right[0], right)
-        lb = shift(to_left[1], left)
-        rb = shift(to_right[1], right)
-        la = shift(to_left[0], left)
-        to_right, to_left = (ra, rb), (la, lb)
-        blocks[half - step], blocks[step] = to_right, to_left
-    theirs = shift(exch, [(i, i ^ half) for i in range(n_inner)])
-    blocks[half // 2] = (shift(to_right[0], right), shift(to_left[1], left))
+    for r in sorted(range(1, half), key=lambda r: (r.bit_count(), r)):
+        down, up = r & -r, 1 << (r.bit_length() - 1)
+        by_low = 0 if r == down else r ^ down
+        by_high = 0 if r == up else r ^ up
+        blocks[r] = (swap(blocks[by_low][0], r ^ by_low), swap(blocks[by_high][1], r ^ by_high))
+    theirs = swap(exch, half)
 
     (far_own,) = call(
         functools.partial(skeleton_kernel, leaf, dim),
@@ -541,7 +574,7 @@
 
     lists, counts = call(
         functools.partial(list_kernel, leaves, n_inner),
-        [i32(2, 2 * leaves * near.shape[1]), i32(2)],
+        [i32(4, 2 * leaves * near.shape[1]), i32(4)],
         (near_rows,),
         [SMEM],
         out_specs=[SMEM, SMEM],
@@ -554,30 +587,37 @@
         ]
 
     per_leaf = 2 * leaf * leaf * 256 * 3
-    (own_sum,) = call(
+    own_sum, own_src, own_chg, own_tgt = call(
         functools.partial(self_kernel, leaf, scale),
-        [f32(rows, LANES)],
+        [f32(rows, LANES)] + [jax.ShapeDtypeStruct((leaves, leaf, 4 * dim), BF16)] * 3,
         (exch, own_low, own_high),
         [VMEM] * 3,
-        tiles(leaves) + tiles(leaves)[:1],
         flops=leaves * per_leaf,
     )
     (targets,) = call(
         functools.partial(target_kernel, leaf, scale),
         [jax.ShapeDtypeStruct((2 * leaves, leaf, 4 * dim), BF16)],
-        (exch, theirs),
+        (own_tgt, theirs),
         [VMEM] * 2,
         flops=1 << 20,
     )
-    early = [0] + [j for step in range(1, half // 2) for j in (half - step, step)]
-    sources = [piece for j in early for piece in blocks[j]]
+    sources = [piece for r in range(1, half - 1) for piece in blocks[r]]
+    held_tiles = [jax.ShapeDtypeStruct(((half - 1) * leaves, leaf, 4 * dim), BF16)] * 2
+    acc, src, chg = call(
+        functools.partial(own_near_kernel, leaf, scale),
+        [f32(rows + leaf, LANES)] + held_tiles,
+        (lists, counts, own_tgt, own_src, own_chg, *sources),
+        [SMEM, SMEM] + [VMEM] * 3 + [HBM] * len(sources),
+        [pltpu.VMEM((piece, LANES), F32)] * len(sources) + [pltpu.SemaphoreType.DMA((len(sources),))],
+        flops=(half - 2) * leaves * per_leaf,
+    )
     (acc,) = call(
         functools.partial(near_kernel, leaf, scale),
         [f32(2 * rows + leaf, LANES)],
-        (lists, counts, targets, *sources),
-        [SMEM, SMEM] + [VMEM] * (1 + len(sources)),
-        tiles(len(early) * leaves),
-        flops=len(early) * 2 * leaves * per_leaf,
+        (lists, counts, targets, src, chg, blocks[half - 1][0], acc),
+        [SMEM, SMEM] + [VMEM] * 3 + [HBM, VMEM],
+        tiles(leaves // 2) + [pltpu.VMEM((piece, LANES), F32), pltpu.SemaphoreType.DMA((1,))],
+        flops=half * leaves * per_leaf,
     )
     others = [held[r] for r in range(1, n_outer)]
     n_blocks = len(others) * leaves
@@ -585,25 +625,30 @@
         functools.partial(far_kernel, n_skel, scale, n_inner, len(others)),
         [f32(rows, LANES)],
         (far_rows, far_own, interp, *others),
-        [SMEM] + [VMEM] * (2 + len(others)),
+        [SMEM] + [HBM] * (2 + len(others)),
         [
             pltpu.VMEM((n_blocks, n_skel, 4 * dim), BF16),
             pltpu.VMEM((n_blocks, n_skel, 2 * LANES), BF16),
             pltpu.VMEM((leaves, n_skel, 4 * dim), BF16),
-        ],
+        ]
+        + [pltpu.VMEM((leaves * fline, LANES), F32)] * (1 + len(others))
+        + [pltpu.VMEM(interp.shape, F32), pltpu.SemaphoreType.DMA((2 + len(others),))],
         flops=leaves * 8 * 2 * n_skel * n_skel * 256 * 3,
     )
     (out,) = call(
         functools.partial(last_kernel, devs, pair, leaf, scale),
         [f32(devs * 2 * pair, LANES)],
-        (lists, counts, pos, targets, *blocks[half // 2], acc, own_sum, far_part, theirs[rows // 2 :]),
-        [SMEM] * 3 + [VMEM] * 7,
+        (lists, counts, pos, targets, blocks[half - 1][1], acc, own_sum, far_part, theirs),
+        [SMEM] * 3 + [VMEM, HBM] + [VMEM] * 3 + [HBM],
         [pltpu.VMEM((2 * rows + leaf, LANES), F32)]
-        + tiles(leaves)
+        + tiles(leaves // 2)
         + [
             pltpu.VMEM((devs, LANES), jnp.int32),
             pltpu.SMEM((devs, LANES), jnp.int32),
             pltpu.SemaphoreType.DMA,
+            pltpu.VMEM((piece, LANES), F32),
+            pltpu.VMEM((devs, LANES), F32),
+            pltpu.SemaphoreType.DMA((2,)),
         ],
         flops=2 * leaves * per_leaf,
     )
@@ -613,7 +658,8 @@
         [f32(rows, LANES)],
         (returned.reshape(devs * 2 * pair, LANES), code),
         [VMEM, SMEM],
-        [pltpu.VMEM((rows, LANES), F32)],
+        [pltpu.VMEM((rows, LANES), F32), pltpu.VMEM((rows, LANES), F32), pltpu.SemaphoreType.DMA((4,))],
+        out_specs=[HBM],
     )
     return final
 

time: 216 us -> 211 us (0.977)
  Pallas kernels: 68.9 us -> 65.5 us
  local copies, waits for them, and re-layouts: 4.44 us -> 1.46 us
    pallas_call x10 -> x11, Pallas kernels: 68.9 us -> 65.5 us  [call(): pl.pallas_call(body, out_shape=outs, in_specs=in_specs, out_specs=out_spe...]
    unnamed x21 -> x17, local copies, waits for them, and re-layouts: 4.29 us -> 1.32 us
  transfers between devices with their start and end apart: 10 -> 10, of which waited for: 2 -> 3; matrix products, arithmetic and copies ran while one was open for 0% -> 0% of each run, Pallas kernels for 20% -> 19%
where the time goes in v3:
time: 211 us; the launch traced here: 210 us
  blocking collectives  103 us (49%)
  Pallas kernels  65.5 us (31%)
  waiting for transfers between devices  32.9 us (16%)
  starting transfers between devices  7.12 us (3%)
    pallas_call x11, Pallas kernels, call(): pl.pallas_call(body, out_shape=outs, in_specs=in_specs, out_specs=out_spe...  65.5 us
    all_to_all x1, blocking collectives, shards(): lax.all_to_all(out.reshape(devs, 2 * pair, LANES), JOINT, 0, 0, tiled=True)  54 us
    all_to_all x1, blocking collectives, shards(): lax.all_to_all(send.reshape(devs, block, LANES), JOINT, 0, 0, tiled=True)  48.9 us
    ppermute x7, waiting for transfers between devices, swap(): return lax.ppermute(x, 'inner', [(i, i ^ bit) for i in range(n_inner)])  32.9 us
    ppermute x7, starting transfers between devices, swap(): return lax.ppermute(x, 'inner', [(i, i ^ bit) for i in range(n_inner)])  6.04 us
  transfers between devices with their start and end apart: 10, of which 3 were waited for; matrix products, arithmetic and copies ran while one was open for 0% of the time, Pallas kernels for 19%

profile of v3, /device:TPU:0, one launch (start us, length us, event | category | flops | bytes accessed | tf_op | source)
XLA Modules:
  0.0 210.2 jit_solution(18332028815574549666)
XLA Ops:
  0.0 8.2 %shard_map.74 = (f32[3328,128]{1,0:T(8,128)}, s32[16,128]{1,0:T(8,128)}) custom-call(s32[16,128]{1,0:T(8,128)} %bitcast.11, f32[64,2048]{1,0:T(8,128)} %bitcast.10, f32[2048,128]{1,0:T(8,128)} %chg_hbm.1), custom_call_target="tpu_custom_call" | custom-call | bytes 3293184 | tf_op jit(solution)/shard_map/pallas_call | solution.py:25
  8.3 48.9 %all_to_all.10 = f32[32,104,128]{2,1,0:T(8,128)S(1)} all-to-all(f32[32,104,128]{2,1,0:T(8,128)} %bitcast.9), channel_id=1, replica_groups=mesh['outer'=4,'inner'=8] {'outer','inner'}, dimensions={0} | all-to-all | bytes 3407872 | tf_op jit(solution)/shard_map/all_to_all | solution.py:531
  57.1 4.6 %shard_map.75 = (f32[1536,128]{1,0:T(8,128)}, f32[1536,128]{1,0:T(8,128)}, f32[2048,128]{1,0:T(8,128)S(1)}, f32[1056,128]{1,0:T(8,128)S(1)}, s32[32,128]{1,0:T(8,128)S(1)}) custom-call(f32[3328,128]{1,0:T(8,128)S(1)} %bitcast.7), custom_call_target="tpu_custom_call" | custom-call | bytes 4882432 | tf_op jit(solution)/shard_map/pallas_call | solution.py:25
  61.9 4.5 %shard_map.80.own_hbm = f32[1536,128]{1,0:T(8,128)S(1)} custom-call(f32[1536,128]{1,0:T(8,128)} %get-tuple-element.26.low_ref, f32[1536,128]{1,0:T(8,128)} %get-tuple-element.27.high_ref, f32[2048,128]{1,0:T(8,128)S(1)} %get-tuple-element.35.pts_ref, f32[2048,256]{1,0:T(8,128)S(1)} %copy-done.1, s32[4,256]{1,0:T(4,128)S(1)} %copy-done.3), custom_call_target="tpu_custom_call" | custom-call | flops 402653184 | bytes 5509120 | tf_op jit(solution)/shard_map/pallas_call | solution.py:25
  66.4 0.6 collective-permute-start.8
  67.0 1.6 collective-permute-start.1
  68.5 1.0 collective-permute-start.4
  69.5 1.9 collective-permute-start.3
  71.4 16.9 %collective-permute-done.theirs_ref.theirs_hbm = f32[1056,128]{1,0:T(8,128)S(1)} collective-permute-done((f32[1056,128]{1,0:T(8,128)S(1)}, f32[1056,128]{1,0:T(8,128)S(1)}, u32[]{:S(2)}, u32[]{:S(2)}) %collective-permute-start) | collective-permute-done | bytes 540704 | tf_op jit(solution)/shard_map/ppermute | solution.py:547
  88.4 0.5 collective-permute-start.9
  89.0 0.1 copy.11
  89.2 11.0 %collective-permute-done.4.rest_2_ = f32[1536,128]{1,0:T(8,128)} collective-permute-done((f32[1536,128]{1,0:T(8,128)}, f32[1536,128]{1,0:T(8,128)}, u32[]{:S(2)}, u32[]{:S(2)}) %collective-permute-start.4) | collective-permute-done | bytes 786464 | tf_op jit(solution)/shard_map/ppermute | solution.py:547
  100.2 1.4 collective-permute-start.6
  101.7 2.5 %shard_map.73 = (s32[4,64]{1,0:T(4,128)S(1)}, s32[4]{0:T(128)S(1)}) custom-call(s32[8,8]{1,0:T(8,128)S(1)} %pad_add_fusion.near_ref), custom_call_target="tpu_custom_call" | custom-call | bytes 1296 | tf_op jit(solution)/shard_map/pallas_call | solution.py:25
  104.3 1.0 copy-done.5
  105.3 5.7 %shard_map.76 = (f32[2048,128]{1,0:T(8,128)S(1)}, bf16[4,512,256]{2,1,0:T(8,128)(2,1)S(1)}, bf16[4,512,256]{2,1,0:T(8,128)(2,1)S(1)}, bf16[4,512,256]{2,1,0:T(8,128)(2,1)S(1)}) custom-call(f32[1056,128]{1,0:T(8,128)S(1)} %copy-done.5, f32[1536,128]{1,0:T(8,128)} %get-tuple-element.26.low_ref, f32[1536,128]{1,0:T(8,128)} %get-tuple-element.27.high_ref), custom_call_target="tpu_custom_call" | custom-call | flops 1610612736 | bytes 6307840 | tf_op jit(solution)/shard_map/pallas_call | solution.py:25
  111.0 1.1 shard_map.77.tgt_ref
  112.2 4.9 %collective-permute-done.5.rest_3_ = f32[1536,128]{1,0:T(8,128)} collective-permute-done((f32[1536,128]{1,0:T(8,128)}, f32[1536,128]{1,0:T(8,128)}, u32[]{:S(2)}, u32[]{:S(2)}) %collective-permute-start.5) | collective-permute-done | bytes 786464 | tf_op jit(solution)/shard_map/ppermute | solution.py:547
  117.1 8.0 %shard_map.78 = (f32[2560,128]{1,0:T(8,128)S(1)}, bf16[12,512,256]{2,1,0:T(8,128)(2,1)S(1)}, bf16[12,512,256]{2,1,0:T(8,128)(2,1)S(1)}) custom-call(s32[4,64]{1,0:T(4,128)S(1)} %get-tuple-element.21.list_ref, s32[4]{0:T(128)S(1)} %get-tuple-element.22.count_ref, bf16[4,512,256]{2,1,0:T(8,128)(2,1)S(1)} %get-tuple-element.28.own_ref.tgt_ref, ...), custom_call_target="tpu_custom_call" | custom-call | flops 3221225472 | bytes 13894672 | tf_op jit(solution)/shard_map/pallas_call | solution.py:25
  125.2 9.4 %shard_map.81.far_ref = f32[2048,128]{1,0:T(8,128)S(1)} custom-call(s32[4,8]{1,0:T(4,128)S(1)} %copy.13.far_rows_ref, f32[1536,128]{1,0:T(8,128)S(1)} %shard_map.80.own_hbm, f32[2048,256]{1,0:T(8,128)S(1)} %copy-done.1, f32[1536,128]{1,0:T(8,128)} %collective-permute-done.7.rest_0_, f32[1536,128]{1,0:T(8,128)} %collective-permute-done.8.rest_1_, ...), custom_call_target="tpu_custom_call" | custom-call | flops 3221225472 | bytes 6291584 | tf_op jit(solution)/shard_map/pallas_call | solution.py:25
  134.6 8.8 %shard_map.79.old_ref = f32[4608,128]{1,0:T(8,128)S(1)} custom-call(s32[4,64]{1,0:T(4,128)S(1)} %get-tuple-element.21.list_ref, s32[4]{0:T(128)S(1)} %get-tuple-element.22.count_ref, bf16[8,512,256]{2,1,0:T(8,128)(2,1)S(1)} %shard_map.77.tgt_ref, bf16[12,512,256]{2,1,0:T(8,128)(2,1)S(1)} %get-tuple-element.31.src_ref, ...), custom_call_target="tpu_custom_call" | custom-call | flops 6442450944 | bytes 12846096 | tf_op jit(solution)/shard_map/pallas_call | solution.py:25
  143.4 6.6 %shard_map.82 = f32[4096,128]{1,0:T(8,128)S(1)} custom-call(s32[4,64]{1,0:T(4,128)S(1)} %get-tuple-element.21.list_ref, s32[4]{0:T(128)S(1)} %get-tuple-element.22.count_ref, s32[32,128]{1,0:T(8,128)S(1)} %get-tuple-element.24.pos_ref, bf16[8,512,256]{2,1,0:T(8,128)(2,1)S(1)} %shard_map.77.tgt_ref, f32[1536,128]{1,0:T(8,128)S(1)} %collective-permute-done.2.piece_hbm, ...), custom_call_target="tpu_custom_call" | custom-call | flops 3221225472 | bytes 9995280 | tf_op jit(solution)/shard_map/pallas_call | solution.py:25
  150.0 54.0 %all_to_all.11 = f32[32,128,128]{2,1,0:T(8,128)S(1)} all-to-all(f32[32,128,128]{2,1,0:T(8,128)S(1)} %bitcast.8), channel_id=1, replica_groups=mesh['outer'=4,'inner'=8] {'outer','inner'}, dimensions={0} | all-to-all | bytes 4194304 | tf_op jit(solution)/shard_map/all_to_all | solution.py:655
  204.1 6.0 %shard_map.83 = f32[2048,128]{1,0:T(8,128)} custom-call(f32[4096,128]{1,0:T(8,128)S(1)} %bitcast.6, s32[16,128]{1,0:T(8,128)S(1)} %copy-done.2), custom_call_target="tpu_custom_call" | custom-call | bytes 3153920 | tf_op jit(solution)/shard_map/pallas_call | solution.py:25
  (29 shorter events, 0.5 us)
Async XLA Ops:
  0.0 89.1 %copy-start = (s32[128,8]{0,1:T(8,128)S(1)}, s32[128,8]{0,1:T(8,128)}, u32[]{:S(2)}) copy-start(s32[128,8]{0,1:T(8,128)} %param.12) | copy-start | bytes 12292
  8.3 53.6 %copy-start.1 = (f32[2048,256]{1,0:T(8,128)S(1)}, f32[2048,256]{1,0:T(8,128)}, u32[]{:S(2)}) copy-start(f32[2048,256]{1,0:T(8,128)} %interp_hbm.1) | copy-start | bytes 6291460
  8.3 53.6 %copy-start.3 = (s32[4,256]{1,0:T(4,128)S(1)}, s32[4,256]{1,0:T(4,128)}, u32[]{:S(2)}) copy-start(s32[4,256]{1,0:T(4,128)} %skel_ref.1) | copy-start | bytes 12292
  61.8 4.6 %copy-start.4 = (f32[1056,128]{1,0:T(8,128)}, f32[1056,128]{1,0:T(8,128)S(1)}, u32[]{:S(2)}) copy-start(f32[1056,128]{1,0:T(8,128)S(1)} %get-tuple-element.25.own_ref) | copy-start | bytes 1622020
  61.8 26.6 %collective-permute-start = (f32[1056,128]{1,0:T(8,128)S(1)}, f32[1056,128]{1,0:T(8,128)S(1)}, u32[]{:S(2)}, u32[]{:S(2)}) collective-permute-start(f32[1056,128]{1,0:T(8,128)S(1)} %get-tuple-element.25.own_ref), channel_id=1, source_target_pairs={{0,4},{1,5},{2,6},{3,7},{4,0},{5,1},{6,2},{7,3},{8,12},{9,13},{10,... | collective-permute-start | bytes 1622024 | tf_op jit(solution)/shard_map/ppermute | solution.py:547
  61.9 27.0 %copy-start.6 = (s32[128,8]{0,1:T(8,128)S(1)}, s32[128,8]{0,1:T(8,128)}, u32[]{:S(2)}) copy-start(s32[128,8]{0,1:T(8,128)} %param.11) | copy-start | bytes 12292
  66.4 22.0 %collective-permute-start.8 = (f32[1536,128]{1,0:T(8,128)S(1)}, f32[1536,128]{1,0:T(8,128)}, u32[]{:S(2)}, u32[]{:S(2)}) collective-permute-start(f32[1536,128]{1,0:T(8,128)S(1)} %shard_map.80.own_hbm), channel_id=1, source_target_pairs={{0,16},{8,24},{16,0},{24,8},{1,17},{9,25},{17,1},{25,9},{2,18},{10... | collective-permute-start | bytes 2359304 | tf_op jit(solution)/shard_map/ppermute | solution.py:571
  67.0 21.4 %collective-permute-start.1 = (f32[1536,128]{1,0:T(8,128)}, f32[1536,128]{1,0:T(8,128)}, u32[]{:S(2)}, u32[]{:S(2)}) collective-permute-start(f32[1536,128]{1,0:T(8,128)} %get-tuple-element.27.high_ref), channel_id=1, source_target_pairs={{0,1},{1,0},{2,3},{3,2},{4,5},{5,4},{6,7},{7,6},{8,9},{9,8},{10,11... | collective-permute-start | bytes 2359304 | tf_op jit(solution)/shard_map/ppermute | solution.py:547
  68.5 31.7 %collective-permute-start.4 = (f32[1536,128]{1,0:T(8,128)}, f32[1536,128]{1,0:T(8,128)}, u32[]{:S(2)}, u32[]{:S(2)}) collective-permute-start(f32[1536,128]{1,0:T(8,128)} %get-tuple-element.26.low_ref), channel_id=1, source_target_pairs={{0,2},{1,3},{2,0},{3,1},{4,6},{5,7},{6,4},{7,5},{8,10},{9,11},{10,... | collective-permute-start | bytes 2359304 | tf_op jit(solution)/shard_map/ppermute | solution.py:547
  69.5 42.6 %collective-permute-start.3 = (f32[1536,128]{1,0:T(8,128)}, f32[1536,128]{1,0:T(8,128)}, u32[]{:S(2)}, u32[]{:S(2)}) collective-permute-start(f32[1536,128]{1,0:T(8,128)} %get-tuple-element.26.low_ref), channel_id=1, source_target_pairs={{0,1},{1,0},{2,3},{3,2},{4,5},{5,4},{6,7},{7,6},{8,9},{9,8},{10,11... | collective-permute-start | bytes 2359304 | tf_op jit(solution)/shard_map/ppermute | solution.py:547
  88.4 28.7 %collective-permute-start.5 = (f32[1536,128]{1,0:T(8,128)}, f32[1536,128]{1,0:T(8,128)}, u32[]{:S(2)}, u32[]{:S(2)}) collective-permute-start(f32[1536,128]{1,0:T(8,128)} %get-tuple-element.27.high_ref), channel_id=1, source_target_pairs={{0,2},{1,3},{2,0},{3,1},{4,6},{5,7},{6,4},{7,5},{8,10},{9,11},{10,... | collective-permute-start | bytes 2359304 | tf_op jit(solution)/shard_map/ppermute | solution.py:547
  88.4 36.8 %collective-permute-start.7 = (f32[1536,128]{1,0:T(8,128)S(1)}, f32[1536,128]{1,0:T(8,128)}, u32[]{:S(2)}, u32[]{:S(2)}) collective-permute-start(f32[1536,128]{1,0:T(8,128)S(1)} %shard_map.80.own_hbm), channel_id=1, source_target_pairs={{0,8},{8,0},{16,24},{24,16},{1,9},{9,1},{17,25},{25,17},{2,10},{10... | collective-permute-start | bytes 2359304 | tf_op jit(solution)/shard_map/ppermute | solution.py:571
  88.4 36.8 %collective-permute-start.9 = (f32[1536,128]{1,0:T(8,128)}, f32[1536,128]{1,0:T(8,128)}, u32[]{:S(2)}, u32[]{:S(2)}) collective-permute-start(f32[1536,128]{1,0:T(8,128)} %collective-permute-done.8.rest_1_), channel_id=1, source_target_pairs={{0,8},{8,0},{16,24},{24,16},{1,9},{9,1},{17,25},{25,17},{2,10},{10... | collective-permute-start | bytes 2359304 | tf_op jit(solution)/shard_map/ppermute | solution.py:571
  100.2 34.3 %collective-permute-start.6 = (f32[1536,128]{1,0:T(8,128)}, f32[1536,128]{1,0:T(8,128)}, u32[]{:S(2)}, u32[]{:S(2)}) collective-permute-start(f32[1536,128]{1,0:T(8,128)} %collective-permute-done.4.rest_2_), channel_id=1, source_target_pairs={{0,1},{1,0},{2,3},{3,2},{4,5},{5,4},{6,7},{7,6},{8,9},{9,8},{10,11... | collective-permute-start | bytes 2359304 | tf_op jit(solution)/shard_map/ppermute | solution.py:547
  104.2 1.0 copy-start.5
  112.1 31.3 %collective-permute-start.2 = (f32[1536,128]{1,0:T(8,128)}, f32[1536,128]{1,0:T(8,128)S(1)}, u32[]{:S(2)}, u32[]{:S(2)}) collective-permute-start(f32[1536,128]{1,0:T(8,128)} %collective-permute-done.1.rest_1_), channel_id=1, source_target_pairs={{0,2},{1,3},{2,0},{3,1},{4,6},{5,7},{6,4},{7,5},{8,10},{9,11},{10,... | collective-permute-start | bytes 2359304 | tf_op jit(solution)/shard_map/ppermute | solution.py:547
  150.0 54.1 %copy-start.2 = (s32[16,128]{1,0:T(8,128)S(1)}, s32[16,128]{1,0:T(8,128)}, u32[]{:S(2)}) copy-start(s32[16,128]{1,0:T(8,128)} %get-tuple-element.36.code_ref) | copy-start | bytes 24580

commit v4 on v3

--- a/solution.py
+++ b/solution.py
@@ -135,17 +135,13 @@
     return q, x - q * n
 
 
-UNROLL = 64
-
-
 def rows_loop(count, body):
-    def step(i, carry):
-        line, part = div_mod(i, LANES // UNROLL)
-        for u in range(UNROLL):
-            body(i * UNROLL + u, line, part * UNROLL + u)
-        return carry
-
-    lax.fori_loop(0, count // UNROLL, step, 0)
+    def step(line, carry):
+        for lane in range(LANES):
+            body(line * LANES + lane, line, lane)
+        return carry
+
+    lax.fori_loop(0, count // LANES, step, 0)
 
 
 def send_kernel(devs, pair, block, order_hbm, pts_hbm, chg_hbm, send_ref, code_ref, ptmp, prow, order_ref, pts_ref, chg_ref, idx_v, idx_s, sem, sems):
@@ -254,12 +250,13 @@
     line = leaf + leaf // 2
     fline = skel + skel // 2
 
-    for g in range(leaves):
-
-        def move(n, line, lane, g=g):
+
+    def gather(g, carry):
+        for n in range(skel):
             stmp[pl.ds(g * skel + n, 1), :] = pts_ref[pl.ds(g * leaf + skel_ref[g, n], 1), :]
-
-        rows_loop(skel, move)
+        return carry
+
+    lax.fori_loop(0, leaves, gather, 0)
     for g in range(leaves):
         hi, lo = split(interp_ref[g * leaf : (g + 1) * leaf, :])
         ref, at = (low_ref, g * line) if g < leaves // 2 else (high_ref, (g - leaves // 2) * line)
@@ -431,12 +428,12 @@
     rows = far_ref.shape[0]
     table = theirs_hbm.at[pl.ds(rows // 2, devs), :]
     copies = start_loads([piece_hbm, table], [held, opos_f], sems)
+    acc[:rows, :] = old_ref[:rows, :] + (self_ref[...] + far_ref[...])
+    acc[rows:, :] = old_ref[rows:, :]
     copies[1].wait()
     opos_v[...] = opos_f[...].astype(jnp.int32)
     copy = pltpu.make_async_copy(opos_v, opos_s, sem)
     copy.start()
-    acc[:rows, :] = old_ref[:rows, :] + (self_ref[...] + far_ref[...])
-    acc[rows:, :] = old_ref[rows:, :]
     load_sources(leaf, scale, (held,), src, chg, 0, copies)
     add_listed(leaf, 3, list_ref, count_ref, tgt_ref, src, chg, acc)
     copy.wait()
@@ -461,15 +458,14 @@
 
     parts = sems.shape[0]
     size = out.shape[0] // parts
-    steps = size // UNROLL
+    steps = size // LANES
     copies = []
     for p in range(parts):
 
-        def step(i, carry):
-            line, part = div_mod(i, LANES // UNROLL)
-            for u in range(UNROLL):
-                row = both[pl.ds(code_ref[line, part * UNROLL + u], 1), :]
-                out[pl.ds(i * UNROLL + u, 1), :] = row
+        def step(line, carry):
+            for lane in range(LANES):
+                row = both[pl.ds(code_ref[line, lane], 1), :]
+                out[pl.ds(line * LANES + lane, 1), :] = row
             return carry
 
         lax.fori_loop(p * steps, (p + 1) * steps, step, 0)

time: 211 us -> 204 us (0.967)
  Pallas kernels: 65.5 us -> 59.1 us
    pallas_call x11, Pallas kernels: 65.5 us -> 59.1 us  [call(): pl.pallas_call(body, out_shape=outs, in_specs=in_specs, out_specs=out_spe...]
where the time goes in v4:
time: 204 us
  blocking collectives  103 us (50%)
  Pallas kernels  59.1 us (29%)
  waiting for transfers between devices  32.9 us (16%)
  starting transfers between devices  7.12 us (3%)
    pallas_call x11, Pallas kernels, call(): pl.pallas_call(body, out_shape=outs, in_specs=in_specs, out_specs=out_spe...  59.1 us
    all_to_all x1, blocking collectives, shards(): lax.all_to_all(out.reshape(devs, 2 * pair, LANES), JOINT, 0, 0, tiled=True)  54 us
    all_to_all x1, blocking collectives, shards(): lax.all_to_all(send.reshape(devs, block, LANES), JOINT, 0, 0, tiled=True)  48.9 us
    ppermute x7, waiting for transfers between devices, swap(): return lax.ppermute(x, 'inner', [(i, i ^ bit) for i in range(n_inner)])  32.9 us
    ppermute x7, starting transfers between devices, swap(): return lax.ppermute(x, 'inner', [(i, i ^ bit) for i in range(n_inner)])  6.04 us
  transfers between devices with their start and end apart: 10, of which 3 were waited for; matrix products, arithmetic and copies ran while one was open for 0% of the time, Pallas kernels for 19%

profile of v4, /device:TPU:0, one launch (start us, length us, event | category | flops | bytes accessed | tf_op | source)
XLA Modules:
  0.0 203.8 jit_solution(12900691727185578787)
XLA Ops:
  0.0 5.4 %shard_map.74 = (f32[3328,128]{1,0:T(8,128)}, s32[16,128]{1,0:T(8,128)}) custom-call(s32[16,128]{1,0:T(8,128)} %bitcast.11, f32[64,2048]{1,0:T(8,128)} %bitcast.10, f32[2048,128]{1,0:T(8,128)} %chg_hbm.1), custom_call_target="tpu_custom_call" | custom-call | bytes 3293184 | tf_op jit(solution)/shard_map/pallas_call | solution.py:25
  5.5 48.9 %all_to_all.10 = f32[32,104,128]{2,1,0:T(8,128)S(1)} all-to-all(f32[32,104,128]{2,1,0:T(8,128)} %bitcast.9), channel_id=1, replica_groups=mesh['outer'=4,'inner'=8] {'outer','inner'}, dimensions={0} | all-to-all | bytes 3407872 | tf_op jit(solution)/shard_map/all_to_all | solution.py:527
  54.3 4.6 %shard_map.75 = (f32[1536,128]{1,0:T(8,128)}, f32[1536,128]{1,0:T(8,128)}, f32[2048,128]{1,0:T(8,128)S(1)}, f32[1056,128]{1,0:T(8,128)S(1)}, s32[32,128]{1,0:T(8,128)S(1)}) custom-call(f32[3328,128]{1,0:T(8,128)S(1)} %bitcast.7), custom_call_target="tpu_custom_call" | custom-call | bytes 4882432 | tf_op jit(solution)/shard_map/pallas_call | solution.py:25
  59.1 3.7 %shard_map.80.own_hbm = f32[1536,128]{1,0:T(8,128)S(1)} custom-call(f32[1536,128]{1,0:T(8,128)} %get-tuple-element.26.low_ref, f32[1536,128]{1,0:T(8,128)} %get-tuple-element.27.high_ref, f32[2048,128]{1,0:T(8,128)S(1)} %get-tuple-element.35.pts_ref, f32[2048,256]{1,0:T(8,128)S(1)} %copy-done.1, s32[4,256]{1,0:T(4,128)S(1)} %copy-done.3), custom_call_target="tpu_custom_call" | custom-call | flops 402653184 | bytes 5509120 | tf_op jit(solution)/shard_map/pallas_call | solution.py:25
  62.7 0.6 collective-permute-start.8
  63.3 1.6 collective-permute-start.1
  64.9 1.0 collective-permute-start.4
  65.9 1.9 collective-permute-start.3
  67.8 17.7 %collective-permute-done.theirs_ref.theirs_hbm = f32[1056,128]{1,0:T(8,128)S(1)} collective-permute-done((f32[1056,128]{1,0:T(8,128)S(1)}, f32[1056,128]{1,0:T(8,128)S(1)}, u32[]{:S(2)}, u32[]{:S(2)}) %collective-permute-start) | collective-permute-done | bytes 540704 | tf_op jit(solution)/shard_map/ppermute | solution.py:543
  85.6 0.5 collective-permute-start.9
  86.2 0.1 copy.11
  86.4 10.2 %collective-permute-done.4.rest_2_ = f32[1536,128]{1,0:T(8,128)} collective-permute-done((f32[1536,128]{1,0:T(8,128)}, f32[1536,128]{1,0:T(8,128)}, u32[]{:S(2)}, u32[]{:S(2)}) %collective-permute-start.4) | collective-permute-done | bytes 786464 | tf_op jit(solution)/shard_map/ppermute | solution.py:543
  96.6 1.4 collective-permute-start.6
  98.1 2.5 %shard_map.73 = (s32[4,64]{1,0:T(4,128)S(1)}, s32[4]{0:T(128)S(1)}) custom-call(s32[8,8]{1,0:T(8,128)S(1)} %pad_add_fusion.near_ref), custom_call_target="tpu_custom_call" | custom-call | bytes 1296 | tf_op jit(solution)/shard_map/pallas_call | solution.py:25
  100.6 1.0 copy-done.5
  101.7 5.7 %shard_map.76 = (f32[2048,128]{1,0:T(8,128)S(1)}, bf16[4,512,256]{2,1,0:T(8,128)(2,1)S(1)}, bf16[4,512,256]{2,1,0:T(8,128)(2,1)S(1)}, bf16[4,512,256]{2,1,0:T(8,128)(2,1)S(1)}) custom-call(f32[1056,128]{1,0:T(8,128)S(1)} %copy-done.5, f32[1536,128]{1,0:T(8,128)} %get-tuple-element.26.low_ref, f32[1536,128]{1,0:T(8,128)} %get-tuple-element.27.high_ref), custom_call_target="tpu_custom_call" | custom-call | flops 1610612736 | bytes 6307840 | tf_op jit(solution)/shard_map/pallas_call | solution.py:25
  107.4 1.1 shard_map.77.tgt_ref
  108.6 4.9 %collective-permute-done.5.rest_3_ = f32[1536,128]{1,0:T(8,128)} collective-permute-done((f32[1536,128]{1,0:T(8,128)}, f32[1536,128]{1,0:T(8,128)}, u32[]{:S(2)}, u32[]{:S(2)}) %collective-permute-start.5) | collective-permute-done | bytes 786464 | tf_op jit(solution)/shard_map/ppermute | solution.py:543
  113.5 8.0 %shard_map.78 = (f32[2560,128]{1,0:T(8,128)S(1)}, bf16[12,512,256]{2,1,0:T(8,128)(2,1)S(1)}, bf16[12,512,256]{2,1,0:T(8,128)(2,1)S(1)}) custom-call(s32[4,64]{1,0:T(4,128)S(1)} %get-tuple-element.21.list_ref, s32[4]{0:T(128)S(1)} %get-tuple-element.22.count_ref, bf16[4,512,256]{2,1,0:T(8,128)(2,1)S(1)} %get-tuple-element.28.own_ref.tgt_ref, ...), custom_call_target="tpu_custom_call" | custom-call | flops 3221225472 | bytes 13894672 | tf_op jit(solution)/shard_map/pallas_call | solution.py:25
  121.5 9.4 %shard_map.81.far_ref = f32[2048,128]{1,0:T(8,128)S(1)} custom-call(s32[4,8]{1,0:T(4,128)S(1)} %copy.13.far_rows_ref, f32[1536,128]{1,0:T(8,128)S(1)} %shard_map.80.own_hbm, f32[2048,256]{1,0:T(8,128)S(1)} %copy-done.1, f32[1536,128]{1,0:T(8,128)} %collective-permute-done.7.rest_0_, f32[1536,128]{1,0:T(8,128)} %collective-permute-done.8.rest_1_, ...), custom_call_target="tpu_custom_call" | custom-call | flops 3221225472 | bytes 6291584 | tf_op jit(solution)/shard_map/pallas_call | solution.py:25
  131.0 8.8 %shard_map.79.old_ref = f32[4608,128]{1,0:T(8,128)S(1)} custom-call(s32[4,64]{1,0:T(4,128)S(1)} %get-tuple-element.21.list_ref, s32[4]{0:T(128)S(1)} %get-tuple-element.22.count_ref, bf16[8,512,256]{2,1,0:T(8,128)(2,1)S(1)} %shard_map.77.tgt_ref, bf16[12,512,256]{2,1,0:T(8,128)(2,1)S(1)} %get-tuple-element.31.src_ref, ...), custom_call_target="tpu_custom_call" | custom-call | flops 6442450944 | bytes 12846096 | tf_op jit(solution)/shard_map/pallas_call | solution.py:25
  139.8 6.5 %shard_map.82 = f32[4096,128]{1,0:T(8,128)S(1)} custom-call(s32[4,64]{1,0:T(4,128)S(1)} %get-tuple-element.21.list_ref, s32[4]{0:T(128)S(1)} %get-tuple-element.22.count_ref, s32[32,128]{1,0:T(8,128)S(1)} %get-tuple-element.24.pos_ref, bf16[8,512,256]{2,1,0:T(8,128)(2,1)S(1)} %shard_map.77.tgt_ref, f32[1536,128]{1,0:T(8,128)S(1)} %collective-permute-done.2.piece_hbm, ...), custom_call_target="tpu_custom_call" | custom-call | flops 3221225472 | bytes 9995280 | tf_op jit(solution)/shard_map/pallas_call | solution.py:25
  146.4 54.0 %all_to_all.11 = f32[32,128,128]{2,1,0:T(8,128)S(1)} all-to-all(f32[32,128,128]{2,1,0:T(8,128)S(1)} %bitcast.8), channel_id=1, replica_groups=mesh['outer'=4,'inner'=8] {'outer','inner'}, dimensions={0} | all-to-all | bytes 4194304 | tf_op jit(solution)/shard_map/all_to_all | solution.py:651
  200.4 3.2 %shard_map.83 = f32[2048,128]{1,0:T(8,128)} custom-call(f32[4096,128]{1,0:T(8,128)S(1)} %bitcast.6, s32[16,128]{1,0:T(8,128)S(1)} %copy-done.2), custom_call_target="tpu_custom_call" | custom-call | bytes 3153920 | tf_op jit(solution)/shard_map/pallas_call | solution.py:25
  (29 shorter events, 0.5 us)
Async XLA Ops:
  0.0 86.3 %copy-start = (s32[128,8]{0,1:T(8,128)S(1)}, s32[128,8]{0,1:T(8,128)}, u32[]{:S(2)}) copy-start(s32[128,8]{0,1:T(8,128)} %param.12) | copy-start | bytes 12292
  5.5 53.6 %copy-start.1 = (f32[2048,256]{1,0:T(8,128)S(1)}, f32[2048,256]{1,0:T(8,128)}, u32[]{:S(2)}) copy-start(f32[2048,256]{1,0:T(8,128)} %interp_hbm.1) | copy-start | bytes 6291460
  5.5 53.6 %copy-start.3 = (s32[4,256]{1,0:T(4,128)S(1)}, s32[4,256]{1,0:T(4,128)}, u32[]{:S(2)}) copy-start(s32[4,256]{1,0:T(4,128)} %skel_ref.1) | copy-start | bytes 12292
  59.0 3.8 %copy-start.4 = (f32[1056,128]{1,0:T(8,128)}, f32[1056,128]{1,0:T(8,128)S(1)}, u32[]{:S(2)}) copy-start(f32[1056,128]{1,0:T(8,128)S(1)} %get-tuple-element.25.own_ref) | copy-start | bytes 1622020
  59.0 26.6 %collective-permute-start = (f32[1056,128]{1,0:T(8,128)S(1)}, f32[1056,128]{1,0:T(8,128)S(1)}, u32[]{:S(2)}, u32[]{:S(2)}) collective-permute-start(f32[1056,128]{1,0:T(8,128)S(1)} %get-tuple-element.25.own_ref), channel_id=1, source_target_pairs={{0,4},{1,5},{2,6},{3,7},{4,0},{5,1},{6,2},{7,3},{8,12},{9,13},{10,... | collective-permute-start | bytes 1622024 | tf_op jit(solution)/shard_map/ppermute | solution.py:543
  59.1 27.0 %copy-start.6 = (s32[128,8]{0,1:T(8,128)S(1)}, s32[128,8]{0,1:T(8,128)}, u32[]{:S(2)}) copy-start(s32[128,8]{0,1:T(8,128)} %param.11) | copy-start | bytes 12292
  62.7 22.8 %collective-permute-start.8 = (f32[1536,128]{1,0:T(8,128)S(1)}, f32[1536,128]{1,0:T(8,128)}, u32[]{:S(2)}, u32[]{:S(2)}) collective-permute-start(f32[1536,128]{1,0:T(8,128)S(1)} %shard_map.80.own_hbm), channel_id=1, source_target_pairs={{0,16},{8,24},{16,0},{24,8},{1,17},{9,25},{17,1},{25,9},{2,18},{10... | collective-permute-start | bytes 2359304 | tf_op jit(solution)/shard_map/ppermute | solution.py:567
  63.3 22.2 %collective-permute-start.1 = (f32[1536,128]{1,0:T(8,128)}, f32[1536,128]{1,0:T(8,128)}, u32[]{:S(2)}, u32[]{:S(2)}) collective-permute-start(f32[1536,128]{1,0:T(8,128)} %get-tuple-element.27.high_ref), channel_id=1, source_target_pairs={{0,1},{1,0},{2,3},{3,2},{4,5},{5,4},{6,7},{7,6},{8,9},{9,8},{10,11... | collective-permute-start | bytes 2359304 | tf_op jit(solution)/shard_map/ppermute | solution.py:543
  64.9 31.7 %collective-permute-start.4 = (f32[1536,128]{1,0:T(8,128)}, f32[1536,128]{1,0:T(8,128)}, u32[]{:S(2)}, u32[]{:S(2)}) collective-permute-start(f32[1536,128]{1,0:T(8,128)} %get-tuple-element.26.low_ref), channel_id=1, source_target_pairs={{0,2},{1,3},{2,0},{3,1},{4,6},{5,7},{6,4},{7,5},{8,10},{9,11},{10,... | collective-permute-start | bytes 2359304 | tf_op jit(solution)/shard_map/ppermute | solution.py:543
  65.9 42.6 %collective-permute-start.3 = (f32[1536,128]{1,0:T(8,128)}, f32[1536,128]{1,0:T(8,128)}, u32[]{:S(2)}, u32[]{:S(2)}) collective-permute-start(f32[1536,128]{1,0:T(8,128)} %get-tuple-element.26.low_ref), channel_id=1, source_target_pairs={{0,1},{1,0},{2,3},{3,2},{4,5},{5,4},{6,7},{7,6},{8,9},{9,8},{10,11... | collective-permute-start | bytes 2359304 | tf_op jit(solution)/shard_map/ppermute | solution.py:543
  85.6 27.9 %collective-permute-start.5 = (f32[1536,128]{1,0:T(8,128)}, f32[1536,128]{1,0:T(8,128)}, u32[]{:S(2)}, u32[]{:S(2)}) collective-permute-start(f32[1536,128]{1,0:T(8,128)} %get-tuple-element.27.high_ref), channel_id=1, source_target_pairs={{0,2},{1,3},{2,0},{3,1},{4,6},{5,7},{6,4},{7,5},{8,10},{9,11},{10,... | collective-permute-start | bytes 2359304 | tf_op jit(solution)/shard_map/ppermute | solution.py:543
  85.6 36.0 %collective-permute-start.7 = (f32[1536,128]{1,0:T(8,128)S(1)}, f32[1536,128]{1,0:T(8,128)}, u32[]{:S(2)}, u32[]{:S(2)}) collective-permute-start(f32[1536,128]{1,0:T(8,128)S(1)} %shard_map.80.own_hbm), channel_id=1, source_target_pairs={{0,8},{8,0},{16,24},{24,16},{1,9},{9,1},{17,25},{25,17},{2,10},{10... | collective-permute-start | bytes 2359304 | tf_op jit(solution)/shard_map/ppermute | solution.py:567
  85.6 36.0 %collective-permute-start.9 = (f32[1536,128]{1,0:T(8,128)}, f32[1536,128]{1,0:T(8,128)}, u32[]{:S(2)}, u32[]{:S(2)}) collective-permute-start(f32[1536,128]{1,0:T(8,128)} %collective-permute-done.8.rest_1_), channel_id=1, source_target_pairs={{0,8},{8,0},{16,24},{24,16},{1,9},{9,1},{17,25},{25,17},{2,10},{10... | collective-permute-start | bytes 2359304 | tf_op jit(solution)/shard_map/ppermute | solution.py:567
  96.6 34.3 %collective-permute-start.6 = (f32[1536,128]{1,0:T(8,128)}, f32[1536,128]{1,0:T(8,128)}, u32[]{:S(2)}, u32[]{:S(2)}) collective-permute-start(f32[1536,128]{1,0:T(8,128)} %collective-permute-done.4.rest_2_), channel_id=1, source_target_pairs={{0,1},{1,0},{2,3},{3,2},{4,5},{5,4},{6,7},{7,6},{8,9},{9,8},{10,11... | collective-permute-start | bytes 2359304 | tf_op jit(solution)/shard_map/ppermute | solution.py:543
  100.6 1.0 copy-start.5
  108.5 31.3 %collective-permute-start.2 = (f32[1536,128]{1,0:T(8,128)}, f32[1536,128]{1,0:T(8,128)S(1)}, u32[]{:S(2)}, u32[]{:S(2)}) collective-permute-start(f32[1536,128]{1,0:T(8,128)} %collective-permute-done.1.rest_1_), channel_id=1, source_target_pairs={{0,2},{1,3},{2,0},{3,1},{4,6},{5,7},{6,4},{7,5},{8,10},{9,11},{10,... | collective-permute-start | bytes 2359304 | tf_op jit(solution)/shard_map/ppermute | solution.py:543
  146.4 54.1 %copy-start.2 = (s32[16,128]{1,0:T(8,128)S(1)}, s32[16,128]{1,0:T(8,128)}, u32[]{:S(2)}) copy-start(s32[16,128]{1,0:T(8,128)} %get-tuple-element.36.code_ref) | copy-start | bytes 24580

commit v5 on v4

--- a/solution.py
+++ b/solution.py
@@ -402,34 +402,33 @@
     lax.fori_loop(0, lax.shift_right_logical(count_ref[row], jnp.int32(GROUP.bit_length() - 1)), entry, 0)
 
 
-def own_near_kernel(leaf, scale, list_ref, count_ref, tgt_ref, src_ref, chg_ref, *rest):
+def own_near_kernel(leaf, scale, list_ref, count_ref, tgt_ref, src_ref, chg_ref, self_ref, *rest):
     n = (len(rest) - 4) // 2
     sources, (acc_ref, src, chg), bufs, sems = rest[:n], rest[n : n + 3], rest[n + 3 : -1], rest[-1]
     copies = start_loads(sources, bufs, sems)
     leaves = src_ref.shape[0]
     src[:leaves] = src_ref[...]
     chg[:leaves] = chg_ref[...]
-    acc_ref[...] = jnp.zeros_like(acc_ref)
+    acc_ref[: self_ref.shape[0], :] = self_ref[...]
     load_sources(leaf, scale, bufs, src, chg, leaves, copies)
     add_listed(leaf, 0, list_ref, count_ref, tgt_ref, src, chg, acc_ref)
 
 
-def near_kernel(leaf, scale, list_ref, count_ref, tgt_ref, src_ref, chg_ref, low_hbm, own_ref, acc_ref, src, chg, low, sems):
+def near_kernel(leaf, scale, list_ref, count_ref, tgt_ref, src_ref, chg_ref, low_hbm, own_ref, far_ref, acc_ref, src, chg, low, sems):
     rows = own_ref.shape[0] - leaf
     copies = start_loads([low_hbm], [low], sems)
-    acc_ref[:rows, :] = own_ref[:rows, :]
+    acc_ref[:rows, :] = own_ref[:rows, :] + far_ref[...]
     acc_ref[rows:, :] = jnp.zeros((acc_ref.shape[0] - rows, LANES), F32)
     add_listed(leaf, 1, list_ref, count_ref, tgt_ref, src_ref, chg_ref, acc_ref)
     load_sources(leaf, scale, (low,), src, chg, 0, copies)
     add_listed(leaf, 2, list_ref, count_ref, tgt_ref, src, chg, acc_ref)
 
 
-def last_kernel(devs, pair, leaf, scale, list_ref, count_ref, pos_ref, tgt_ref, piece_hbm, old_ref, self_ref, far_ref, theirs_hbm, out_ref, acc, src, chg, opos_v, opos_s, sem, held, opos_f, sems):
-    rows = far_ref.shape[0]
+def last_kernel(devs, pair, leaf, scale, list_ref, count_ref, pos_ref, tgt_ref, piece_hbm, old_ref, theirs_hbm, out_ref, acc, src, chg, opos_v, opos_s, sem, held, opos_f, sems):
+    rows = (acc.shape[0] - leaf) // 2
     table = theirs_hbm.at[pl.ds(rows // 2, devs), :]
     copies = start_loads([piece_hbm, table], [held, opos_f], sems)
-    acc[:rows, :] = old_ref[:rows, :] + (self_ref[...] + far_ref[...])
-    acc[rows:, :] = old_ref[rows:, :]
+    acc[...] = old_ref[...]
     copies[1].wait()
     opos_v[...] = opos_f[...].astype(jnp.int32)
     copy = pltpu.make_async_copy(opos_v, opos_s, sem)
@@ -597,24 +596,6 @@
         [VMEM] * 2,
         flops=1 << 20,
     )
-    sources = [piece for r in range(1, half - 1) for piece in blocks[r]]
-    held_tiles = [jax.ShapeDtypeStruct(((half - 1) * leaves, leaf, 4 * dim), BF16)] * 2
-    acc, src, chg = call(
-        functools.partial(own_near_kernel, leaf, scale),
-        [f32(rows + leaf, LANES)] + held_tiles,
-        (lists, counts, own_tgt, own_src, own_chg, *sources),
-        [SMEM, SMEM] + [VMEM] * 3 + [HBM] * len(sources),
-        [pltpu.VMEM((piece, LANES), F32)] * len(sources) + [pltpu.SemaphoreType.DMA((len(sources),))],
-        flops=(half - 2) * leaves * per_leaf,
-    )
-    (acc,) = call(
-        functools.partial(near_kernel, leaf, scale),
-        [f32(2 * rows + leaf, LANES)],
-        (lists, counts, targets, src, chg, blocks[half - 1][0], acc),
-        [SMEM, SMEM] + [VMEM] * 3 + [HBM, VMEM],
-        tiles(leaves // 2) + [pltpu.VMEM((piece, LANES), F32), pltpu.SemaphoreType.DMA((1,))],
-        flops=half * leaves * per_leaf,
-    )
     others = [held[r] for r in range(1, n_outer)]
     n_blocks = len(others) * leaves
     (far_part,) = call(
@@ -631,11 +612,29 @@
         + [pltpu.VMEM(interp.shape, F32), pltpu.SemaphoreType.DMA((2 + len(others),))],
         flops=leaves * 8 * 2 * n_skel * n_skel * 256 * 3,
     )
+    sources = [piece for r in range(1, half - 1) for piece in blocks[r]]
+    held_tiles = [jax.ShapeDtypeStruct(((half - 1) * leaves, leaf, 4 * dim), BF16)] * 2
+    acc, src, chg = call(
+        functools.partial(own_near_kernel, leaf, scale),
+        [f32(rows + leaf, LANES)] + held_tiles,
+        (lists, counts, own_tgt, own_src, own_chg, own_sum, *sources),
+        [SMEM, SMEM] + [VMEM] * 4 + [HBM] * len(sources),
+        [pltpu.VMEM((piece, LANES), F32)] * len(sources) + [pltpu.SemaphoreType.DMA((len(sources),))],
+        flops=(half - 2) * leaves * per_leaf,
+    )
+    (acc,) = call(
+        functools.partial(near_kernel, leaf, scale),
+        [f32(2 * rows + leaf, LANES)],
+        (lists, counts, targets, src, chg, blocks[half - 1][0], acc, far_part),
+        [SMEM, SMEM] + [VMEM] * 3 + [HBM, VMEM, VMEM],
+        tiles(leaves // 2) + [pltpu.VMEM((piece, LANES), F32), pltpu.SemaphoreType.DMA((1,))],
+        flops=half * leaves * per_leaf,
+    )
     (out,) = call(
         functools.partial(last_kernel, devs, pair, leaf, scale),
         [f32(devs * 2 * pair, LANES)],
-        (lists, counts, pos, targets, blocks[half - 1][1], acc, own_sum, far_part, theirs),
-        [SMEM] * 3 + [VMEM, HBM] + [VMEM] * 3 + [HBM],
+        (lists, counts, pos, targets, blocks[half - 1][1], acc, theirs),
+        [SMEM] * 3 + [VMEM, HBM, VMEM, HBM],
         [pltpu.VMEM((2 * rows + leaf, LANES), F32)]
         + tiles(leaves // 2)
         + [

time: 204 us -> 204 us (level)
  no operation moved by 1% of the time
where the time goes in v5:
time: 204 us
  blocking collectives  103 us (50%)
  Pallas kernels  59 us (29%)
  waiting for transfers between devices  32.9 us (16%)
  starting transfers between devices  7.12 us (3%)
    pallas_call x11, Pallas kernels, call(): pl.pallas_call(body, out_shape=outs, in_specs=in_specs, out_specs=out_spe...  59 us
    all_to_all x1, blocking collectives, shards(): lax.all_to_all(out.reshape(devs, 2 * pair, LANES), JOINT, 0, 0, tiled=True)  54 us
    all_to_all x1, blocking collectives, shards(): lax.all_to_all(send.reshape(devs, block, LANES), JOINT, 0, 0, tiled=True)  48.9 us
    ppermute x7, waiting for transfers between devices, swap(): return lax.ppermute(x, 'inner', [(i, i ^ bit) for i in range(n_inner)])  32.9 us
    ppermute x7, starting transfers between devices, swap(): return lax.ppermute(x, 'inner', [(i, i ^ bit) for i in range(n_inner)])  6.04 us
  transfers between devices with their start and end apart: 10, of which 3 were waited for; matrix products, arithmetic and copies ran while one was open for 0% of the time, Pallas kernels for 19%

profile of v5, /device:TPU:0, one launch (start us, length us, event | category | flops | bytes accessed | tf_op | source)
XLA Modules:
  0.0 203.7 jit_solution(4747095881988880393)
XLA Ops:
  0.0 5.4 %shard_map.74 = (f32[3328,128]{1,0:T(8,128)}, s32[16,128]{1,0:T(8,128)}) custom-call(s32[16,128]{1,0:T(8,128)} %bitcast.11, f32[64,2048]{1,0:T(8,128)} %bitcast.10, f32[2048,128]{1,0:T(8,128)} %chg_hbm.1), custom_call_target="tpu_custom_call" | custom-call | bytes 3293184 | tf_op jit(solution)/shard_map/pallas_call | solution.py:25
  5.5 48.9 %all_to_all.10 = f32[32,104,128]{2,1,0:T(8,128)S(1)} all-to-all(f32[32,104,128]{2,1,0:T(8,128)} %bitcast.9), channel_id=1, replica_groups=mesh['outer'=4,'inner'=8] {'outer','inner'}, dimensions={0} | all-to-all | bytes 3407872 | tf_op jit(solution)/shard_map/all_to_all | solution.py:526
  54.3 4.6 %shard_map.75 = (f32[1536,128]{1,0:T(8,128)}, f32[1536,128]{1,0:T(8,128)}, f32[2048,128]{1,0:T(8,128)S(1)}, f32[1056,128]{1,0:T(8,128)S(1)}, s32[32,128]{1,0:T(8,128)S(1)}) custom-call(f32[3328,128]{1,0:T(8,128)S(1)} %bitcast.7), custom_call_target="tpu_custom_call" | custom-call | bytes 4882432 | tf_op jit(solution)/shard_map/pallas_call | solution.py:25
  59.1 3.7 %shard_map.79.own_hbm = f32[1536,128]{1,0:T(8,128)S(1)} custom-call(f32[1536,128]{1,0:T(8,128)} %get-tuple-element.26.low_ref, f32[1536,128]{1,0:T(8,128)} %get-tuple-element.27.high_ref, f32[2048,128]{1,0:T(8,128)S(1)} %get-tuple-element.35.pts_ref, f32[2048,256]{1,0:T(8,128)S(1)} %copy-done.1, s32[4,256]{1,0:T(4,128)S(1)} %copy-done.3), custom_call_target="tpu_custom_call" | custom-call | flops 402653184 | bytes 5509120 | tf_op jit(solution)/shard_map/pallas_call | solution.py:25
  62.7 0.6 collective-permute-start.8
  63.3 1.6 collective-permute-start.1
  64.9 1.0 collective-permute-start.4
  65.9 1.9 collective-permute-start.3
  67.8 17.7 %collective-permute-done.theirs_ref.theirs_hbm = f32[1056,128]{1,0:T(8,128)S(1)} collective-permute-done((f32[1056,128]{1,0:T(8,128)S(1)}, f32[1056,128]{1,0:T(8,128)S(1)}, u32[]{:S(2)}, u32[]{:S(2)}) %collective-permute-start) | collective-permute-done | bytes 540704 | tf_op jit(solution)/shard_map/ppermute | solution.py:542
  85.6 0.5 collective-permute-start.9
  86.2 0.1 copy.11
  86.4 10.2 %collective-permute-done.4.rest_2_ = f32[1536,128]{1,0:T(8,128)} collective-permute-done((f32[1536,128]{1,0:T(8,128)}, f32[1536,128]{1,0:T(8,128)}, u32[]{:S(2)}, u32[]{:S(2)}) %collective-permute-start.4) | collective-permute-done | bytes 786464 | tf_op jit(solution)/shard_map/ppermute | solution.py:542
  96.6 1.4 collective-permute-start.6
  98.1 2.5 %shard_map.73 = (s32[4,64]{1,0:T(4,128)S(1)}, s32[4]{0:T(128)S(1)}) custom-call(s32[8,8]{1,0:T(8,128)S(1)} %pad_add_fusion.near_ref), custom_call_target="tpu_custom_call" | custom-call | bytes 1296 | tf_op jit(solution)/shard_map/pallas_call | solution.py:25
  100.6 1.0 copy-done.5
  101.7 5.7 %shard_map.76 = (f32[2048,128]{1,0:T(8,128)S(1)}, bf16[4,512,256]{2,1,0:T(8,128)(2,1)S(1)}, bf16[4,512,256]{2,1,0:T(8,128)(2,1)S(1)}, bf16[4,512,256]{2,1,0:T(8,128)(2,1)S(1)}) custom-call(f32[1056,128]{1,0:T(8,128)S(1)} %copy-done.5, f32[1536,128]{1,0:T(8,128)} %get-tuple-element.26.low_ref, f32[1536,128]{1,0:T(8,128)} %get-tuple-element.27.high_ref), custom_call_target="tpu_custom_call" | custom-call | flops 1610612736 | bytes 6307840 | tf_op jit(solution)/shard_map/pallas_call | solution.py:25
  107.4 1.1 shard_map.77.tgt_ref
  108.6 4.9 %collective-permute-done.5.rest_3_ = f32[1536,128]{1,0:T(8,128)} collective-permute-done((f32[1536,128]{1,0:T(8,128)}, f32[1536,128]{1,0:T(8,128)}, u32[]{:S(2)}, u32[]{:S(2)}) %collective-permute-start.5) | collective-permute-done | bytes 786464 | tf_op jit(solution)/shard_map/ppermute | solution.py:542
  113.5 8.0 %shard_map.78 = (f32[2560,128]{1,0:T(8,128)S(1)}, bf16[12,512,256]{2,1,0:T(8,128)(2,1)S(1)}, bf16[12,512,256]{2,1,0:T(8,128)(2,1)S(1)}) custom-call(s32[4,64]{1,0:T(4,128)S(1)} %get-tuple-element.21.list_ref, s32[4]{0:T(128)S(1)} %get-tuple-element.22.count_ref, bf16[4,512,256]{2,1,0:T(8,128)(2,1)S(1)} %get-tuple-element.28.own_ref.tgt_ref, ...), custom_call_target="tpu_custom_call" | custom-call | flops 3221225472 | bytes 14943248 | tf_op jit(solution)/shard_map/pallas_call | solution.py:25
  121.5 9.4 %shard_map.80.far_ref = f32[2048,128]{1,0:T(8,128)S(1)} custom-call(s32[4,8]{1,0:T(4,128)S(1)} %copy.13.far_rows_ref, f32[1536,128]{1,0:T(8,128)S(1)} %shard_map.79.own_hbm, f32[2048,256]{1,0:T(8,128)S(1)} %copy-done.1, f32[1536,128]{1,0:T(8,128)} %collective-permute-done.7.rest_0_, f32[1536,128]{1,0:T(8,128)} %collective-permute-done.8.rest_1_, ...), custom_call_target="tpu_custom_call" | custom-call | flops 3221225472 | bytes 6291584 | tf_op jit(solution)/shard_map/pallas_call | solution.py:25
  131.0 8.9 %shard_map.81.old_ref = f32[4608,128]{1,0:T(8,128)S(1)} custom-call(s32[4,64]{1,0:T(4,128)S(1)} %get-tuple-element.21.list_ref, s32[4]{0:T(128)S(1)} %get-tuple-element.22.count_ref, bf16[8,512,256]{2,1,0:T(8,128)(2,1)S(1)} %shard_map.77.tgt_ref, bf16[12,512,256]{2,1,0:T(8,128)(2,1)S(1)} %get-tuple-element.32.src_ref, ...), custom_call_target="tpu_custom_call" | custom-call | flops 6442450944 | bytes 13894672 | tf_op jit(solution)/shard_map/pallas_call | solution.py:25
  139.9 6.4 %shard_map.82 = f32[4096,128]{1,0:T(8,128)S(1)} custom-call(s32[4,64]{1,0:T(4,128)S(1)} %get-tuple-element.21.list_ref, s32[4]{0:T(128)S(1)} %get-tuple-element.22.count_ref, s32[32,128]{1,0:T(8,128)S(1)} %get-tuple-element.24.pos_ref, bf16[8,512,256]{2,1,0:T(8,128)(2,1)S(1)} %shard_map.77.tgt_ref, f32[1536,128]{1,0:T(8,128)S(1)} %collective-permute-done.2.piece_hbm, ...), custom_call_target="tpu_custom_call" | custom-call | flops 3221225472 | bytes 7898128 | tf_op jit(solution)/shard_map/pallas_call | solution.py:25
  146.3 54.0 %all_to_all.11 = f32[32,128,128]{2,1,0:T(8,128)S(1)} all-to-all(f32[32,128,128]{2,1,0:T(8,128)S(1)} %bitcast.8), channel_id=1, replica_groups=mesh['outer'=4,'inner'=8] {'outer','inner'}, dimensions={0} | all-to-all | bytes 4194304 | tf_op jit(solution)/shard_map/all_to_all | solution.py:650
  200.3 3.2 %shard_map.83 = f32[2048,128]{1,0:T(8,128)} custom-call(f32[4096,128]{1,0:T(8,128)S(1)} %bitcast.6, s32[16,128]{1,0:T(8,128)S(1)} %copy-done.2), custom_call_target="tpu_custom_call" | custom-call | bytes 3153920 | tf_op jit(solution)/shard_map/pallas_call | solution.py:25
  (29 shorter events, 0.5 us)
Async XLA Ops:
  0.0 86.3 %copy-start = (s32[128,8]{0,1:T(8,128)S(1)}, s32[128,8]{0,1:T(8,128)}, u32[]{:S(2)}) copy-start(s32[128,8]{0,1:T(8,128)} %param.12) | copy-start | bytes 12292
  5.5 53.6 %copy-start.1 = (f32[2048,256]{1,0:T(8,128)S(1)}, f32[2048,256]{1,0:T(8,128)}, u32[]{:S(2)}) copy-start(f32[2048,256]{1,0:T(8,128)} %interp_hbm.1) | copy-start | bytes 6291460
  5.5 53.6 %copy-start.3 = (s32[4,256]{1,0:T(4,128)S(1)}, s32[4,256]{1,0:T(4,128)}, u32[]{:S(2)}) copy-start(s32[4,256]{1,0:T(4,128)} %skel_ref.1) | copy-start | bytes 12292
  59.0 3.8 %copy-start.4 = (f32[1056,128]{1,0:T(8,128)}, f32[1056,128]{1,0:T(8,128)S(1)}, u32[]{:S(2)}) copy-start(f32[1056,128]{1,0:T(8,128)S(1)} %get-tuple-element.25.own_ref) | copy-start | bytes 1622020
  59.0 26.6 %collective-permute-start = (f32[1056,128]{1,0:T(8,128)S(1)}, f32[1056,128]{1,0:T(8,128)S(1)}, u32[]{:S(2)}, u32[]{:S(2)}) collective-permute-start(f32[1056,128]{1,0:T(8,128)S(1)} %get-tuple-element.25.own_ref), channel_id=1, source_target_pairs={{0,4},{1,5},{2,6},{3,7},{4,0},{5,1},{6,2},{7,3},{8,12},{9,13},{10,... | collective-permute-start | bytes 1622024 | tf_op jit(solution)/shard_map/ppermute | solution.py:542
  59.1 27.0 %copy-start.6 = (s32[128,8]{0,1:T(8,128)S(1)}, s32[128,8]{0,1:T(8,128)}, u32[]{:S(2)}) copy-start(s32[128,8]{0,1:T(8,128)} %param.11) | copy-start | bytes 12292
  62.7 22.8 %collective-permute-start.8 = (f32[1536,128]{1,0:T(8,128)S(1)}, f32[1536,128]{1,0:T(8,128)}, u32[]{:S(2)}, u32[]{:S(2)}) collective-permute-start(f32[1536,128]{1,0:T(8,128)S(1)} %shard_map.79.own_hbm), channel_id=1, source_target_pairs={{0,16},{8,24},{16,0},{24,8},{1,17},{9,25},{17,1},{25,9},{2,18},{10... | collective-permute-start | bytes 2359304 | tf_op jit(solution)/shard_map/ppermute | solution.py:566
  63.3 22.2 %collective-permute-start.1 = (f32[1536,128]{1,0:T(8,128)}, f32[1536,128]{1,0:T(8,128)}, u32[]{:S(2)}, u32[]{:S(2)}) collective-permute-start(f32[1536,128]{1,0:T(8,128)} %get-tuple-element.27.high_ref), channel_id=1, source_target_pairs={{0,1},{1,0},{2,3},{3,2},{4,5},{5,4},{6,7},{7,6},{8,9},{9,8},{10,11... | collective-permute-start | bytes 2359304 | tf_op jit(solution)/shard_map/ppermute | solution.py:542
  64.9 31.7 %collective-permute-start.4 = (f32[1536,128]{1,0:T(8,128)}, f32[1536,128]{1,0:T(8,128)}, u32[]{:S(2)}, u32[]{:S(2)}) collective-permute-start(f32[1536,128]{1,0:T(8,128)} %get-tuple-element.26.low_ref), channel_id=1, source_target_pairs={{0,2},{1,3},{2,0},{3,1},{4,6},{5,7},{6,4},{7,5},{8,10},{9,11},{10,... | collective-permute-start | bytes 2359304 | tf_op jit(solution)/shard_map/ppermute | solution.py:542
  65.9 42.6 %collective-permute-start.3 = (f32[1536,128]{1,0:T(8,128)}, f32[1536,128]{1,0:T(8,128)}, u32[]{:S(2)}, u32[]{:S(2)}) collective-permute-start(f32[1536,128]{1,0:T(8,128)} %get-tuple-element.26.low_ref), channel_id=1, source_target_pairs={{0,1},{1,0},{2,3},{3,2},{4,5},{5,4},{6,7},{7,6},{8,9},{9,8},{10,11... | collective-permute-start | bytes 2359304 | tf_op jit(solution)/shard_map/ppermute | solution.py:542
  85.6 27.9 %collective-permute-start.5 = (f32[1536,128]{1,0:T(8,128)}, f32[1536,128]{1,0:T(8,128)}, u32[]{:S(2)}, u32[]{:S(2)}) collective-permute-start(f32[1536,128]{1,0:T(8,128)} %get-tuple-element.27.high_ref), channel_id=1, source_target_pairs={{0,2},{1,3},{2,0},{3,1},{4,6},{5,7},{6,4},{7,5},{8,10},{9,11},{10,... | collective-permute-start | bytes 2359304 | tf_op jit(solution)/shard_map/ppermute | solution.py:542
  85.6 36.0 %collective-permute-start.7 = (f32[1536,128]{1,0:T(8,128)S(1)}, f32[1536,128]{1,0:T(8,128)}, u32[]{:S(2)}, u32[]{:S(2)}) collective-permute-start(f32[1536,128]{1,0:T(8,128)S(1)} %shard_map.79.own_hbm), channel_id=1, source_target_pairs={{0,8},{8,0},{16,24},{24,16},{1,9},{9,1},{17,25},{25,17},{2,10},{10... | collective-permute-start | bytes 2359304 | tf_op jit(solution)/shard_map/ppermute | solution.py:566
  85.6 36.0 %collective-permute-start.9 = (f32[1536,128]{1,0:T(8,128)}, f32[1536,128]{1,0:T(8,128)}, u32[]{:S(2)}, u32[]{:S(2)}) collective-permute-start(f32[1536,128]{1,0:T(8,128)} %collective-permute-done.8.rest_1_), channel_id=1, source_target_pairs={{0,8},{8,0},{16,24},{24,16},{1,9},{9,1},{17,25},{25,17},{2,10},{10... | collective-permute-start | bytes 2359304 | tf_op jit(solution)/shard_map/ppermute | solution.py:566
  96.6 34.3 %collective-permute-start.6 = (f32[1536,128]{1,0:T(8,128)}, f32[1536,128]{1,0:T(8,128)}, u32[]{:S(2)}, u32[]{:S(2)}) collective-permute-start(f32[1536,128]{1,0:T(8,128)} %collective-permute-done.4.rest_2_), channel_id=1, source_target_pairs={{0,1},{1,0},{2,3},{3,2},{4,5},{5,4},{6,7},{7,6},{8,9},{9,8},{10,11... | collective-permute-start | bytes 2359304 | tf_op jit(solution)/shard_map/ppermute | solution.py:542
  100.6 1.0 copy-start.5
  108.5 31.3 %collective-permute-start.2 = (f32[1536,128]{1,0:T(8,128)}, f32[1536,128]{1,0:T(8,128)S(1)}, u32[]{:S(2)}, u32[]{:S(2)}) collective-permute-start(f32[1536,128]{1,0:T(8,128)} %collective-permute-done.1.rest_1_), channel_id=1, source_target_pairs={{0,2},{1,3},{2,0},{3,1},{4,6},{5,7},{6,4},{7,5},{8,10},{9,11},{10,... | collective-permute-start | bytes 2359304 | tf_op jit(solution)/shard_map/ppermute | solution.py:542
  146.3 54.1 %copy-start.2 = (s32[16,128]{1,0:T(8,128)S(1)}, s32[16,128]{1,0:T(8,128)}, u32[]{:S(2)}) copy-start(s32[16,128]{1,0:T(8,128)} %get-tuple-element.36.code_ref) | copy-start | bytes 24580
